TPU v7x, 32 devices: a whole 2x2x4 slice. The times are simulated.
32 devices in a mesh: aa: 16 (over z, x, core), ba: 2 (over y).
Axes of the slice: x: 2, y: 2, z: 4, core: 2. Of those that a mesh axis runs over, the one named last changes fastest.
Arguments:
- bev_query: bfloat16 [64, 512, 256], P('aa', 'ba'), may hold values from -6 to 6
- features: bfloat16 [1536, 256], P(('aa', 'ba')), may hold values from -6 to 6
- camera_ids: int32 [64, 512, 8], P('aa', 'ba'), may hold values from 0 to 11
- level_ids: int32 [64, 512, 8], P('aa', 'ba'), may hold values from 0 to 3
- sample_index: int32 [64, 512, 8], P('aa', 'ba'), may hold values from 0 to 31
- sample_weight: bfloat16 [64, 512, 8, 8], P('aa', 'ba'), may hold values from 0 to 0.5
- value_weight: bfloat16 [256, 256], replicated, may hold values from -0.375 to 0.375
- cross_weight: bfloat16 [256, 256], replicated, may hold values from -0.375 to 0.375
- row_project: bfloat16 [256, 768], replicated, may hold values from -3 to 3
- row_output: bfloat16 [256, 256], replicated, may hold values from -0.375 to 0.375
- column_project: bfloat16 [256, 768], replicated, may hold values from -3 to 3
- column_output: bfloat16 [256, 256], replicated, may hold values from -0.375 to 0.375
- expand_weight: bfloat16 [256, 512], replicated, may hold values from -0.375 to 0.375
- reduce_weight: bfloat16 [512, 256], replicated, may hold values from -0.25 to 0.25
- norm_gains: float32 [4, 256], replicated, may hold values from 0.25 to 1.75
Outputs:
- encoded: bfloat16 [64, 512, 256], P('aa', 'ba')
All inputs are finite; a program needn't handle non-finite values.
Results may differ from a plain program's by a relative error of at most 0.015.
Values may be sent and summed in bfloat16 or wider, within the bound.
No kernel may reach another device: no remote copies, remote signals or barrier semaphores. Data moves between devices by JAX's collectives and lax.ppermute only.
A program may use at most 128 MiB of HBM per device.

v0:
```python
import math

import jax
import jax.numpy as jnp
from jax import lax
from jax.sharding import PartitionSpec as P

C = 256
HEADS = 8
CAMS = 12
LEVELS = 4


def layer_norm(values, gain):
    average = jnp.mean(values, -1, keepdims=True)
    centred = values - average
    spread = jnp.mean(centred * centred, -1, keepdims=True)
    return centred * lax.rsqrt(spread + 1e-05) * gain


def matmul(left, right):
    return jnp.dot(left, right, preferred_element_type=jnp.float32)


def attend(query, keys, values):
    head_size = C // HEADS
    head_count = query.shape[-1] // head_size
    query_heads = query.reshape(query.shape[0], head_count, head_size)
    key_heads = keys.reshape(keys.shape[0], head_count, head_size)
    value_heads = values.reshape(values.shape[0], head_count, head_size)
    scores = jnp.einsum(
        "qhd,khd->hqk", query_heads, key_heads, preferred_element_type=jnp.float32
    ) * (1.0 / math.sqrt(head_size))
    weights_bf = jax.nn.softmax(scores, -1).astype(jnp.bfloat16)
    result = jnp.einsum("hqk,khd->qhd", weights_bf, value_heads, preferred_element_type=jnp.float32)
    return result.reshape(query.shape[0], head_count * head_size).astype(jnp.bfloat16)


def blend(value_table, flat_rows, weights):
    head_count = weights.shape[2]
    channels = value_table.shape[1]
    picked = jnp.take(value_table, flat_rows, axis=0)
    picked = picked.reshape(
        flat_rows.shape[0],
        flat_rows.shape[1],
        flat_rows.shape[2],
        head_count,
        channels // head_count,
    )
    blended = jnp.einsum("rwshd,rwhs->rwhd", picked, weights, preferred_element_type=jnp.float32)
    return blended.reshape(flat_rows.shape[0], flat_rows.shape[1], channels).astype(jnp.bfloat16)


def per_device(
    bev_query,
    features,
    camera_ids,
    level_ids,
    sample_index,
    sample_weight,
    value_weight,
    cross_weight,
    row_project,
    row_output,
    column_project,
    column_output,
    expand_weight,
    reduce_weight,
    norm_gains,
):
    band_count = lax.axis_size("aa")
    group_count = lax.axis_size("ba")
    map_cells = features.shape[0] * band_count * group_count // (CAMS * LEVELS)
    value_rows = matmul(features, value_weight).astype(jnp.bfloat16)
    flat_rows = (camera_ids * LEVELS + level_ids) * map_cells + sample_index
    value_table = lax.all_gather(value_rows, ("aa", "ba"), axis=0, tiled=True)
    sampled = blend(value_table, flat_rows, sample_weight)
    summed = bev_query.astype(jnp.float32) + matmul(sampled, cross_weight)
    after_cross = layer_norm(summed, norm_gains[0]).astype(jnp.bfloat16)
    projected = matmul(after_cross, row_project).astype(jnp.bfloat16)
    stacked = projected.reshape(projected.shape[0], projected.shape[1], 3, C)

    def one_row(parts):
        return attend(parts[:, 0], parts[:, 1], parts[:, 2])

    attended = lax.map(
        one_row, lax.all_to_all(stacked, "ba", split_axis=3, concat_axis=1, tiled=True)
    )
    row_mixed = lax.all_to_all(attended, "ba", split_axis=1, concat_axis=2, tiled=True)
    summed = after_cross.astype(jnp.float32) + matmul(row_mixed, row_output)
    after_rows = layer_norm(summed, norm_gains[1]).astype(jnp.bfloat16)
    local_rows = after_rows.shape[0]
    local_cols = after_rows.shape[1]
    grouped = after_rows.reshape(local_rows, band_count, local_cols // band_count, C)
    column_block = lax.all_to_all(grouped, "aa", split_axis=1, concat_axis=0, tiled=True)
    grid_rows = column_block.shape[0]
    column_count = column_block.shape[2]
    lines = column_block.reshape(grid_rows, column_count, C)
    projected_cols = matmul(lines, column_project).astype(jnp.bfloat16)
    ordered = jnp.swapaxes(projected_cols, 0, 1)

    def one_column(line):
        return attend(line[:, :C], line[:, C : 2 * C], line[:, 2 * C :])

    column_mixed = jnp.swapaxes(lax.map(one_column, ordered), 0, 1)
    total = lines.astype(jnp.float32) + matmul(column_mixed, column_output)
    after_columns = layer_norm(total, norm_gains[2]).astype(jnp.bfloat16)
    hidden = jax.nn.relu(matmul(after_columns, expand_weight)).astype(jnp.bfloat16)
    total = after_columns.astype(jnp.float32) + matmul(hidden, reduce_weight)
    encoded_lines = layer_norm(total, norm_gains[3]).astype(jnp.bfloat16)
    encoded_cols = encoded_lines.reshape(grid_rows, 1, column_count, C)
    returned = lax.all_to_all(encoded_cols, "aa", split_axis=0, concat_axis=1, tiled=True)
    return returned.reshape(local_rows, local_cols, C)


def solution(mesh):
    in_specs = (
        P("aa", "ba", None),
        P(("aa", "ba"), None),
        P("aa", "ba", None),
        P("aa", "ba", None),
        P("aa", "ba", None),
        P("aa", "ba", None, None),
        P(),
        P(),
        P(),
        P(),
        P(),
        P(),
        P(),
        P(),
        P(),
    )
    out_specs = P("aa", "ba", None)
    return jax.shard_map(
        per_device, mesh=mesh, in_specs=in_specs, out_specs=out_specs, check_vma=False
    )
```

profile of v0, /device:TPU:0, one launch (start us, length us, event | category | flops | bytes accessed | tf_op | source)
XLA Modules:
  0.0 296.9 jit_solution(10271432234753977156)
XLA Ops:
  2.4 74.0 %all_gather.3 = bf16[1536,256]{1,0:T(8,128)(2,1)S(1)} all-gather(bf16[48,256]{1,0:T(8,128)(2,1)S(1)} %convolution_convert_fusion.3), channel_id=1, replica_groups=mesh['aa'=16,'ba'=2] {'aa','ba'}, dimensions={0}, use_global_device_ids=true | all-gather | bytes 811008 | tf_op jit(solution)/shard_map/all_gather | solution.py:76
  76.4 32.9 %gather_fusion = bf16[8192,256]{1,0:T(8,128)(2,1)} fusion(bf16[1536,256]{1,0:T(8,128)(2,1)S(1)} %all_gather.3, s32[8192]{0:T(1024)S(1)} %broadcast_clamp_fusion), kind=kCustom, calls=%fused_computation | custom fusion | bytes 8421376 | tf_op jit(solution)/shard_map/jit(_take)/gather | solution.py:42
  109.2 18.7 %gather.7 = bf16[4,256,8,8,32]{4,3,2,1,0:T(8,128)(2,1)} reshape(bf16[8192,256]{1,0:T(8,128)(2,1)} %gather_fusion) | data formatting | bytes 8388608 | tf_op jit(solution)/shard_map/jit(_take)/gather | solution.py:42
  128.3 2.4 copy.109
  130.7 22.3 %multiply_reduce_fusion.1 = bf16[4,256,8,32]{3,2,1,0:T(8,128)(2,1)S(1)} fusion(f32[4,256,8,8]{2,3,1,0:T(8,128)} %copy.109, bf16[4,256,8,8,32]{4,3,2,1,0:T(8,128)(2,1)} %gather.7, pred[4,256,8]{2,1,0:T(8,128)(4,1)S(1)} %copy.73), kind=kLoop, calls=%fused_computation.23 | loop fusion | flops 8126464 | bytes 4988928
  156.4 1.9 convolution_convert_fusion.2
  160.1 2.4 copy.77
  162.4 3.7 %all-to-all-start = ((bf16[4,256,3,256]{1,0,2,3:T(4,128)(2,1)}), bf16[4,256,3,256]{1,0,2,3:T(4,128)(2,1)S(1)}, u32[]{:S(2)}, u32[]{:S(2)}) async-start(bf16[4,256,3,256]{1,0,2,3:T(4,128)(2,1)} %copy.77), calls=%async_computation | async-start | bytes 3145728 | tf_op jit(solution)/shard_map/all_to_all | solution.py:87
  166.1 16.7 %all-to-all-done = bf16[4,256,3,256]{1,0,2,3:T(4,128)(2,1)S(1)} async-done(((bf16[4,256,3,256]{1,0,2,3:T(4,128)(2,1)}), bf16[4,256,3,256]{1,0,2,3:T(4,128)(2,1)S(1)}, u32[]{:S(2)}, u32[]{:S(2)}) %all-to-all-start) | async-done | bytes 1572896 | tf_op jit(solution)/shard_map/all_to_all | solution.py:87
  184.2 2.6 copy.79
  186.8 29.5 %while.20 = (s32[]{:T(128)}, bf16[4,512,128]{1,2,0:T(8,128)(2,1)S(1)}, bf16[4,512,3,128]{3,1,2,0:T(8,128)(2,1)}, s32[]{:T(128)}) while((s32[]{:T(128)}, bf16[4,512,128]{1,2,0:T(8,128)(2,1)S(1)}, bf16[4,512,3,128]{3,1,2,0:T(8,128)(2,1)}, s32[]{:T(128)}) %tuple.62), condition=%wide.region_5.6_spmd, body=%wide.region_2.0_spmd.sunk | while | flops 139526656 | bytes 11550781 | solution.py:86
  188.1 3.4 %fusion.70 = (f32[4,512]{1,0:T(4,128)S(1)}, f32[4,512,512]{1,2,0:T(8,128)}) fusion(bf16[512,4,32]{0,2,1:T(8,128)(2,1)S(1)} %bitcast.145, bf16[512,4,32]{0,2,1:T(8,128)(2,1)S(1)} %bitcast.144), kind=kOutput, calls=%fused_computation.66.clone.1 | convolution fusion | flops 70255104 | bytes 4464640 | tf_op jit(solution)/shard_map/while/body/eval_jaxpr/sub | solution.py:34
  191.5 2.7 fusion.71
  195.4 3.4 %fusion.70 = (f32[4,512]{1,0:T(4,128)S(1)}, f32[4,512,512]{1,2,0:T(8,128)}) fusion(bf16[512,4,32]{0,2,1:T(8,128)(2,1)S(1)} %bitcast.145, bf16[512,4,32]{0,2,1:T(8,128)(2,1)S(1)} %bitcast.144), kind=kOutput, calls=%fused_computation.66.clone.1 | convolution fusion | flops 70255104 | bytes 4464640 | tf_op jit(solution)/shard_map/while/body/eval_jaxpr/sub | solution.py:34
  198.9 2.7 fusion.71
  202.8 3.4 %fusion.70 = (f32[4,512]{1,0:T(4,128)S(1)}, f32[4,512,512]{1,2,0:T(8,128)}) fusion(bf16[512,4,32]{0,2,1:T(8,128)(2,1)S(1)} %bitcast.145, bf16[512,4,32]{0,2,1:T(8,128)(2,1)S(1)} %bitcast.144), kind=kOutput, calls=%fused_computation.66.clone.1 | convolution fusion | flops 70255104 | bytes 4464640 | tf_op jit(solution)/shard_map/while/body/eval_jaxpr/sub | solution.py:34
  206.3 2.7 fusion.71
  210.2 3.4 %fusion.70 = (f32[4,512]{1,0:T(4,128)S(1)}, f32[4,512,512]{1,2,0:T(8,128)}) fusion(bf16[512,4,32]{0,2,1:T(8,128)(2,1)S(1)} %bitcast.145, bf16[512,4,32]{0,2,1:T(8,128)(2,1)S(1)} %bitcast.144), kind=kOutput, calls=%fused_computation.66.clone.1 | convolution fusion | flops 70255104 | bytes 4464640 | tf_op jit(solution)/shard_map/while/body/eval_jaxpr/sub | solution.py:34
  213.6 2.7 fusion.71
  216.7 9.0 %all_to_all.66 = bf16[4,512,128]{2,0,1:T(4,128)(2,1)S(1)} all-to-all(bf16[4,512,128]{2,0,1:T(4,128)(2,1)S(1)} %copy.81), channel_id=1, replica_groups=mesh['aa'=16,'ba'=2] {'ba'}, dimensions={1} | all-to-all | bytes 1048576 | tf_op jit(solution)/shard_map/all_to_all | solution.py:89
  228.7 3.6 %all-to-all-start.2 = ((bf16[4,16,16,256]{3,2,0,1:T(8,128)(2,1)}), bf16[4,16,16,256]{3,2,0,1:T(8,128)(2,1)S(1)}, u32[]{:S(2)}, u32[]{:S(2)}) async-start(bf16[4,16,16,256]{3,2,0,1:T(8,128)(2,1)} %copy.83), calls=%async_computation.2 | async-start | bytes 1048576 | tf_op jit(solution)/shard_map/all_to_all | solution.py:95
  232.3 14.2 %all-to-all-done.2 = bf16[4,16,16,256]{3,2,0,1:T(8,128)(2,1)S(1)} async-done(((bf16[4,16,16,256]{3,2,0,1:T(8,128)(2,1)}), bf16[4,16,16,256]{3,2,0,1:T(8,128)(2,1)S(1)}, u32[]{:S(2)}, u32[]{:S(2)}) %all-to-all-start.2) | async-done | bytes 524320 | tf_op jit(solution)/shard_map/all_to_all | solution.py:95
  247.2 25.0 %while.21 = (s32[]{:T(128)}, bf16[16,64,256]{1,2,0:T(8,128)(2,1)}, bf16[16,64,768]{2,1,0:T(8,128)(2,1)S(1)}, s32[]{:T(128)}) while((s32[]{:T(128)}, bf16[16,64,256]{1,2,0:T(8,128)(2,1)}, bf16[16,64,768]{2,1,0:T(8,128)(2,1)S(1)}, s32[]{:T(128)}) %tuple.59), condition=%wide.region_11.12_spmd, body=%wide.region_8.11_spmd.sunk | while | flops 6537856 | bytes 1151545 | solution.py:105
  277.9 18.2 %all_to_all.67 = bf16[64,1,16,256]{3,2,1,0:T(8,128)(2,1)S(1)} all-to-all(bf16[64,1,16,256]{3,2,1,0:T(8,128)(2,1)S(1)} %copy.90), channel_id=1, replica_groups=mesh['aa'=16,'ba'=2] {'aa'}, dimensions={0} | all-to-all | bytes 1048576 | tf_op jit(solution)/shard_map/all_to_all | solution.py:112
  (191 shorter events, 49.1 us)
Async XLA Ops:
  0.0 156.4 %copy-start = (bf16[256,768]{1,0:T(8,128)(2,1)S(1)}, bf16[256,768]{1,0:T(8,128)(2,1)}, u32[]{:S(2)}) copy-start(bf16[256,768]{1,0:T(8,128)(2,1)} %param.27) | copy-start | bytes 1179652
  109.2 19.0 %copy-start.4 = (bf16[4,256,8,8]{1,3,2,0:T(8,128)(2,1)S(1)}, bf16[4,256,8,8]{1,3,2,0:T(8,128)(2,1)}, u32[]{:S(2)}) copy-start(bf16[4,256,8,8]{1,3,2,0:T(8,128)(2,1)} %param.24) | copy-start | bytes 393220
  130.7 23.4 %copy-start.1 = (bf16[4,256,256]{2,1,0:T(8,128)(2,1)S(1)}, bf16[4,256,256]{2,1,0:T(8,128)(2,1)}, u32[]{:S(2)}) copy-start(bf16[4,256,256]{2,1,0:T(8,128)(2,1)} %param.19) | copy-start | bytes 1572868
  152.9 2.9 copy-start.7
  162.4 20.4 %all-to-all-start = ((bf16[4,256,3,256]{1,0,2,3:T(4,128)(2,1)}), bf16[4,256,3,256]{1,0,2,3:T(4,128)(2,1)S(1)}, u32[]{:S(2)}, u32[]{:S(2)}) async-start(bf16[4,256,3,256]{1,0,2,3:T(4,128)(2,1)} %copy.77), calls=%async_computation | async-start | bytes 3145728 | tf_op jit(solution)/shard_map/all_to_all | solution.py:87
  216.3 10.2 %copy-start.5 = (bf16[256,256]{1,0:T(8,128)(2,1)S(1)}, bf16[256,256]{1,0:T(8,128)(2,1)}, u32[]{:S(2)}) copy-start(bf16[256,256]{1,0:T(8,128)(2,1)} %param.28) | copy-start | bytes 393220
  216.3 11.2 %copy-start.10 = (f32[1,256]{1,0:T(1,128)S(1)}, f32[1,256]{1,0:T(1,128)}, u32[]{:S(2)}) copy-start(f32[1,256]{1,0:T(1,128)} %get-tuple-element.82) | copy-start | bytes 3076
  226.2 20.4 %copy-start.2 = (bf16[256,768]{1,0:T(8,128)(2,1)S(1)}, bf16[256,768]{1,0:T(8,128)(2,1)}, u32[]{:S(2)}) copy-start(bf16[256,768]{1,0:T(8,128)(2,1)} %param.29) | copy-start | bytes 1179652
  228.7 17.8 %all-to-all-start.2 = ((bf16[4,16,16,256]{3,2,0,1:T(8,128)(2,1)}), bf16[4,16,16,256]{3,2,0,1:T(8,128)(2,1)S(1)}, u32[]{:S(2)}, u32[]{:S(2)}) async-start(bf16[4,16,16,256]{3,2,0,1:T(8,128)(2,1)} %copy.83), calls=%async_computation.2 | async-start | bytes 1048576 | tf_op jit(solution)/shard_map/all_to_all | solution.py:95
  247.2 25.0 %copy-start.6 = (bf16[256,256]{1,0:T(8,128)(2,1)S(1)}, bf16[256,256]{1,0:T(8,128)(2,1)}, u32[]{:S(2)}) copy-start(bf16[256,256]{1,0:T(8,128)(2,1)} %param.30) | copy-start | bytes 393220
  247.2 27.4 %copy-start.9 = (f32[1,256]{1,0:T(1,128)S(1)}, f32[1,256]{1,0:T(1,128)}, u32[]{:S(2)}) copy-start(f32[1,256]{1,0:T(1,128)} %get-tuple-element.84) | copy-start | bytes 3076
  272.2 2.7 copy-start.11
  272.2 3.2 %copy-start.3 = (bf16[512,256]{1,0:T(8,128)(2,1)S(1)}, bf16[512,256]{1,0:T(8,128)(2,1)}, u32[]{:S(2)}) copy-start(bf16[512,256]{1,0:T(8,128)(2,1)} %param.32) | copy-start | bytes 786436
  274.1 3.1 %copy-start.8 = (f32[1,256]{1,0:T(1,128)S(1)}, f32[1,256]{1,0:T(1,128)}, u32[]{:S(2)}) copy-start(f32[1,256]{1,0:T(1,128)} %get-tuple-element.81) | copy-start | bytes 3076
where the time goes:
time: 298 us; the launch traced here: 297 us
  blocking collectives  101 us (34%)
  local copies, waits for them, and re-layouts  85.8 us (29%)
  matrix products  45 us (15%)
  waiting for transfers between devices  31 us (10%)
  other arithmetic  25.8 us (9%)
  starting transfers between devices  7.24 us (2%)
    all_gather x1, blocking collectives, per_device(): value_table = lax.all_gather(value_rows, ('aa', 'ba'), axis=0, tiled=True)  74 us
    gather x2, local copies, waits for them, and re-layouts, blend(): picked = jnp.take(value_table, flat_rows, axis=0)  51.6 us
    unnamed x1, other arithmetic  22.3 us
    sub x20, matrix products, attend(): weights_bf = jax.nn.softmax(scores, -1).astype(jnp.bfloat16)  18.5 us
    all_to_all x1, blocking collectives, per_device(): lax.all_to_all(encoded_cols, 'aa', split_axis=0, concat_axis=1, tiled=True)  18.2 us
    all_to_all x1, waiting for transfers between devices, per_device(): lax.all_to_all(stacked, 'ba', split_axis=3, concat_axis=1, tiled=True)  16.7 us
    all_to_all x1, waiting for transfers between devices, per_device(): lax.all_to_all(grouped, 'aa', split_axis=1, concat_axis=0, tiled=True)  14.2 us
    dot_general x20, matrix products, attend(): jnp.einsum('hqk,khd->qhd', weights_bf, value_heads, preferred_element_typ...  13.6 us
  transfers between devices with their start and end apart: 2, of which 2 were waited for; matrix products, arithmetic and copies ran while one was open for 0% of the time, Pallas kernels for 0%

commit v1 on v0

--- a/solution.py
+++ b/solution.py
@@ -1,14 +1,21 @@
+import functools
 import math
 
 import jax
 import jax.numpy as jnp
 from jax import lax
+from jax.experimental import pallas as pl
+from jax.experimental.pallas import tpu as pltpu
 from jax.sharding import PartitionSpec as P
 
 C = 256
 HEADS = 8
 CAMS = 12
 LEVELS = 4
+HEAD = C // HEADS
+SAMPLES = 8
+LANES = 128
+SCALE = math.log2(math.e) / math.sqrt(HEAD)
 
 
 def layer_norm(values, gain):
@@ -23,35 +30,28 @@
 
 
 def attend(query, keys, values):
-    head_size = C // HEADS
-    head_count = query.shape[-1] // head_size
-    query_heads = query.reshape(query.shape[0], head_count, head_size)
-    key_heads = keys.reshape(keys.shape[0], head_count, head_size)
-    value_heads = values.reshape(values.shape[0], head_count, head_size)
+    head_count = query.shape[-1] // HEAD
+    query_heads = query.reshape(query.shape[0], head_count, HEAD)
+    key_heads = keys.reshape(keys.shape[0], head_count, HEAD)
+    value_heads = values.reshape(values.shape[0], head_count, HEAD)
     scores = jnp.einsum(
         "qhd,khd->hqk", query_heads, key_heads, preferred_element_type=jnp.float32
-    ) * (1.0 / math.sqrt(head_size))
+    ) * (1.0 / math.sqrt(HEAD))
     weights_bf = jax.nn.softmax(scores, -1).astype(jnp.bfloat16)
     result = jnp.einsum("hqk,khd->qhd", weights_bf, value_heads, preferred_element_type=jnp.float32)
-    return result.reshape(query.shape[0], head_count * head_size).astype(jnp.bfloat16)
+    return result.reshape(query.shape[0], head_count * HEAD).astype(jnp.bfloat16)
 
 
 def blend(value_table, flat_rows, weights):
     head_count = weights.shape[2]
     channels = value_table.shape[1]
     picked = jnp.take(value_table, flat_rows, axis=0)
-    picked = picked.reshape(
-        flat_rows.shape[0],
-        flat_rows.shape[1],
-        flat_rows.shape[2],
-        head_count,
-        channels // head_count,
-    )
+    picked = picked.reshape(*flat_rows.shape, head_count, channels // head_count)
     blended = jnp.einsum("rwshd,rwhs->rwhd", picked, weights, preferred_element_type=jnp.float32)
     return blended.reshape(flat_rows.shape[0], flat_rows.shape[1], channels).astype(jnp.bfloat16)
 
 
-def per_device(
+def general_device(
     bev_query,
     features,
     camera_ids,
@@ -113,6 +113,337 @@
     return returned.reshape(local_rows, local_cols, C)
 
 
+def project(weight, cells):
+    return lax.dot_general(
+        weight, cells, (((0,), (0,)), ((), ())), preferred_element_type=jnp.float32
+    )
+
+
+def norm_columns(values, gain):
+    average = jnp.mean(values, 0, keepdims=True)
+    centred = values - average
+    spread = jnp.mean(centred * centred, 0, keepdims=True)
+    return centred * lax.rsqrt(spread + 1e-05) * gain
+
+
+def with_ones(values):
+    return jnp.concatenate([values, jnp.ones((16, values.shape[1]), values.dtype)], 0)
+
+
+def row_kernel(
+    slot_ref,
+    *refs,
+    piece_count,
+    table_count,
+):
+    bev_refs = refs[:piece_count]
+    spot_refs = refs[piece_count : 2 * piece_count]
+    weight_refs = refs[2 * piece_count : 3 * piece_count]
+    refs = refs[3 * piece_count :]
+    table_refs = refs[:table_count]
+    (
+        value_weight_ref,
+        cross_ref,
+        project_ref,
+        output_ref,
+        gains_ref,
+        out_ref,
+        table_scratch,
+    ) = refs[table_count:]
+
+    @pl.when(pl.program_id(0) == 0)
+    def _():
+        start = 0
+        for table_ref in table_refs:
+            rows = table_ref.shape[0]
+            table_scratch[:, start : start + rows] = lax.dot_general(
+                value_weight_ref[...],
+                table_ref[...],
+                (((0,), (1,)), ((), ())),
+                preferred_element_type=jnp.float32,
+            ).astype(jnp.bfloat16)
+            start += rows
+
+    width = bev_refs[0].shape[1]
+    cells = piece_count * width
+    table = table_scratch[...]
+    entries = table.shape[1]
+    spots = jnp.concatenate([ref[0] for ref in spot_refs], -1)
+    weights = jnp.concatenate([ref[0] for ref in weight_refs], -1).astype(jnp.float32)
+    line = lax.broadcasted_iota(jnp.int32, (entries, cells), 0)
+    sampled = [None] * HEADS
+    for s in range(SAMPLES):
+        chosen = jnp.where(line == spots[s : s + 1, :], 1.0, 0.0).astype(jnp.bfloat16)
+        picked = jnp.dot(table, chosen, preferred_element_type=jnp.float32)
+        for h in range(HEADS):
+            row = h * SAMPLES + s
+            term = picked[h * HEAD : (h + 1) * HEAD] * weights[row : row + 1, :]
+            sampled[h] = term if s == 0 else sampled[h] + term
+    sampled = jnp.concatenate([part.astype(jnp.bfloat16) for part in sampled], 0)
+    bev = jnp.concatenate([ref[0].astype(jnp.float32).T for ref in bev_refs], -1)
+    after_cross = norm_columns(
+        bev + project(cross_ref[...], sampled), gains_ref[:, 0:1]
+    ).astype(jnp.bfloat16)
+    projected = project(project_ref[...], after_cross)
+    query = (projected[:C] * SCALE).astype(jnp.bfloat16)
+    keys = projected[C : 2 * C].astype(jnp.bfloat16)
+    values = projected[2 * C :].astype(jnp.bfloat16)
+    mixed = []
+    for h in range(HEADS):
+        span = slice(h * HEAD, (h + 1) * HEAD)
+        scores = project(keys[span], query[span])
+        powers = jnp.exp2(scores - jnp.max(scores, 0, keepdims=True)).astype(jnp.bfloat16)
+        product = jnp.dot(with_ones(values[span]), powers, preferred_element_type=jnp.float32)
+        mixed.append((product[:HEAD] / product[HEAD : HEAD + 1]).astype(jnp.bfloat16))
+    mixed = jnp.concatenate(mixed, 0)
+    summed = after_cross.astype(jnp.float32) + project(output_ref[...], mixed)
+    after_rows = norm_columns(summed, gains_ref[:, 1:2])
+    for piece in range(piece_count):
+        part = after_rows[:, piece * width : (piece + 1) * width].T.astype(jnp.bfloat16)
+        blocks = part.reshape(out_ref.shape[0], out_ref.shape[3], C)
+        out_ref[:, pl.ds(slot_ref[piece], 1), 0] = blocks[:, None]
+
+
+def column_kernel(
+    lines_ref,
+    project_ref,
+    output_ref,
+    expand_ref,
+    reduce_ref,
+    gains_ref,
+    out_ref,
+    cells_scratch,
+    *,
+    column_count,
+):
+    total = lines_ref.shape[0]
+    rows = total // column_count
+    tiles = range(0, C, LANES)
+    for tile, start in enumerate(tiles):
+        cells_scratch[tile] = lines_ref[:, start : start + LANES].astype(jnp.float32)
+    cells = jnp.concatenate(
+        [
+            jnp.concatenate(
+                [
+                    cells_scratch[tile, pl.ds(column, rows, stride=column_count), :]
+                    for column in range(column_count)
+                ],
+                0,
+            ).T
+            for tile in range(len(tiles))
+        ],
+        0,
+    )
+    cells_bf = cells.astype(jnp.bfloat16)
+    projected = project(project_ref[...], cells_bf)
+    query = (projected[:C] * SCALE).astype(jnp.bfloat16)
+    keys = projected[C : 2 * C].astype(jnp.bfloat16)
+    values = projected[2 * C :].astype(jnp.bfloat16)
+    group = max(1, LANES // rows)
+    span = group * rows
+    owner = lax.broadcasted_iota(jnp.int32, (rows, span), 1) // rows
+    spots = [
+        (slice(h * HEAD, (h + 1) * HEAD), slice(start, start + span))
+        for h in range(HEADS)
+        for start in range(0, total, span)
+    ]
+    scores = []
+    for spot in spots:
+        full = project(keys[spot], query[spot])
+        kept = full[:rows]
+        for member in range(1, group):
+            kept = jnp.where(owner == member, full[member * rows : (member + 1) * rows], kept)
+        scores.append(kept)
+    powers = [
+        jnp.exp2(score - jnp.max(score, 0, keepdims=True)) for score in scores
+    ]
+    mixed = []
+    for spot, power in zip(spots, powers):
+        spread = jnp.concatenate(
+            [jnp.where(owner == member, power, 0.0) for member in range(group)], 0
+        ).astype(jnp.bfloat16)
+        product = jnp.dot(with_ones(values[spot]), spread, preferred_element_type=jnp.float32)
+        mixed.append((product[:HEAD] / product[HEAD : HEAD + 1]).astype(jnp.bfloat16))
+    count = total // span
+    mixed = jnp.concatenate(
+        [jnp.concatenate(mixed[h * count : (h + 1) * count], 1) for h in range(HEADS)], 0
+    )
+    after_columns = norm_columns(
+        cells + project(output_ref[...], mixed), gains_ref[:, 2:3]
+    ).astype(jnp.bfloat16)
+    hidden = jnp.maximum(project(expand_ref[...], after_columns), 0.0).astype(jnp.bfloat16)
+    summed = after_columns.astype(jnp.float32) + project(reduce_ref[...], hidden)
+    encoded = norm_columns(summed, gains_ref[:, 3:4]).T
+    for tile, start in enumerate(tiles):
+        for column in range(column_count):
+            cells_scratch[tile, pl.ds(column, rows, stride=column_count), :] = encoded[
+                column * rows : (column + 1) * rows, start : start + LANES
+            ]
+        out_ref[:, start : start + LANES] = cells_scratch[tile].astype(jnp.bfloat16)
+
+
+def exchange_order(band_count, group_count):
+    cores, rest = 2, band_count // 2
+    sides = 2
+    deep = rest // sides
+    first = [k * cores * sides * group_count for k in range(deep)]
+    second = [
+        kx * cores * group_count + ky for ky in range(group_count) for kx in range(sides)
+    ]
+    third = [kc * group_count for kc in range(cores)]
+    return first, second, third
+
+
+def fast_device(
+    bev_query,
+    features,
+    camera_ids,
+    level_ids,
+    sample_index,
+    sample_weight,
+    value_weight,
+    cross_weight,
+    row_project,
+    row_output,
+    column_project,
+    column_output,
+    expand_weight,
+    reduce_weight,
+    norm_gains,
+):
+    band_count = lax.axis_size("aa")
+    group_count = lax.axis_size("ba")
+    device_count = band_count * group_count
+    axes = ("aa", "ba")
+    group = lax.axis_index("ba")
+    me = lax.axis_index("aa") * group_count + group
+    feature_rows = features.shape[0]
+    map_cells = feature_rows * device_count // (CAMS * LEVELS)
+    local_rows, width = bev_query.shape[:2]
+    kept_rows = local_rows // group_count
+    column_count = width // band_count
+
+    maps = jnp.swapaxes(camera_ids * LEVELS + level_ids, 1, 2).astype(jnp.bfloat16)
+    cells = jnp.swapaxes(sample_index, 1, 2).astype(jnp.bfloat16)
+    weights = sample_weight.transpose(0, 2, 3, 1).reshape(local_rows, HEADS * SAMPLES, width)
+
+    def rows_for(member):
+        parts = []
+        for array in (bev_query, weights, maps, cells):
+            block = lax.dynamic_slice_in_dim(array, member * kept_rows, kept_rows, 0)
+            parts.append(block)
+        return parts
+
+    def pack(parts):
+        return jnp.concatenate([part.reshape(-1, C) for part in parts], 0)
+
+    own_parts = rows_for(group)
+    pieces = [own_parts]
+    for offset in range(1, group_count):
+        sent = pack(rows_for(group ^ offset))
+        got = lax.ppermute(sent, "ba", [(i, i ^ offset) for i in range(group_count)])
+        parts, start = [], 0
+        for part in own_parts:
+            rows = part.size // C
+            parts.append(got[start : start + rows].reshape(part.shape))
+            start += rows
+        pieces.append(parts)
+
+    stages = exchange_order(band_count, group_count)
+
+    def send(array, offset):
+        return lax.ppermute(array, axes, [(i, i ^ offset) for i in range(device_count)])
+
+    held = features
+    for offsets in stages[:2]:
+        held = jnp.concatenate([held] + [send(held, offset) for offset in offsets[1:]], 0)
+    tables = [held] + [send(held, offset) for offset in stages[2][1:]]
+
+    order = [0]
+    for offsets in stages:
+        order = [base ^ offset for offset in offsets for base in order]
+    place_of = [0] * device_count
+    for place, offset in enumerate(order):
+        place_of[offset] = place
+
+    def spots_of(parts):
+        flat = parts[2].astype(jnp.int32) * map_cells + parts[3].astype(jnp.int32)
+        offset = (flat // feature_rows) ^ me
+        place = jnp.zeros_like(offset)
+        for bit in range(device_count.bit_length() - 1):
+            place = place + ((offset >> bit) & 1) * place_of[1 << bit]
+        return place * feature_rows + flat % feature_rows
+
+    slots = jnp.stack([group ^ offset for offset in range(group_count)]).astype(jnp.int32)
+    gains = norm_gains.T
+    whole = pl.BlockSpec(memory_space=pltpu.VMEM)
+
+    def per_row(array):
+        return pl.BlockSpec((1,) + array.shape[1:], lambda i: (i, 0, 0))
+
+    bev_pieces = [parts[0] for parts in pieces]
+    spot_pieces = [spots_of(parts) for parts in pieces]
+    weight_pieces = [parts[1] for parts in pieces]
+    sent_shape = (band_count, group_count, kept_rows, column_count, C)
+    after_rows = pl.pallas_call(
+        functools.partial(
+            row_kernel, piece_count=group_count, table_count=len(tables)
+        ),
+        out_shape=jax.ShapeDtypeStruct(sent_shape, jnp.bfloat16),
+        grid=(kept_rows,),
+        in_specs=[pl.BlockSpec(memory_space=pltpu.SMEM)]
+        + [per_row(array) for array in bev_pieces + spot_pieces + weight_pieces]
+        + [whole] * (len(tables) + 5),
+        out_specs=pl.BlockSpec(
+            (band_count, group_count, 1, column_count, C), lambda i: (0, 0, i, 0, 0)
+        ),
+        scratch_shapes=[pltpu.VMEM((C, feature_rows * device_count), jnp.bfloat16)],
+        compiler_params=pltpu.CompilerParams(vmem_limit_bytes=56 * 1024 * 1024),
+        name="rows",
+    )(
+        slots,
+        *bev_pieces,
+        *spot_pieces,
+        *weight_pieces,
+        *tables,
+        value_weight,
+        cross_weight,
+        row_project,
+        row_output,
+        gains,
+    )
+    lines = lax.all_to_all(
+        after_rows.reshape(device_count, kept_rows * column_count, C), axes, 0, 0, tiled=True
+    ).reshape(-1, C)
+    encoded = pl.pallas_call(
+        functools.partial(column_kernel, column_count=column_count),
+        out_shape=jax.ShapeDtypeStruct(lines.shape, jnp.bfloat16),
+        in_specs=[whole] * 6,
+        out_specs=whole,
+        scratch_shapes=[pltpu.VMEM((C // LANES, lines.shape[0], LANES), jnp.float32)],
+        compiler_params=pltpu.CompilerParams(vmem_limit_bytes=56 * 1024 * 1024),
+        name="columns",
+    )(lines, column_project, column_output, expand_weight, reduce_weight, gains)
+    returned = lax.all_to_all(
+        encoded.reshape(band_count, local_rows, column_count, C), "aa", 0, 0, tiled=True
+    )
+    return jnp.swapaxes(returned, 0, 1).reshape(local_rows, width, C)
+
+
+def fits(mesh, bev_query):
+    band_count, group_count = mesh.shape["aa"], mesh.shape["ba"]
+    rows, columns = bev_query.shape[:2]
+    local_rows, width = rows // band_count, columns // group_count
+    return (
+        band_count in (8, 16)
+        and group_count in (2, 4)
+        and local_rows % group_count == 0
+        and width % C == 0
+        and width % (16 * band_count) == 0
+        and rows in (32, 64, 128)
+    )
+
+
 def solution(mesh):
     in_specs = (
         P("aa", "ba", None),
@@ -132,6 +463,11 @@
         P(),
     )
     out_specs = P("aa", "ba", None)
-    return jax.shard_map(
-        per_device, mesh=mesh, in_specs=in_specs, out_specs=out_specs, check_vma=False
-    )
+
+    def encode(*args):
+        body = fast_device if fits(mesh, args[0]) else general_device
+        return jax.shard_map(
+            body, mesh=mesh, in_specs=in_specs, out_specs=out_specs, check_vma=False
+        )(*args)
+
+    return encode

time: 298 us -> 95.6 us (0.32)
  local copies, waits for them, and re-layouts: 85.8 us -> 7.69 us
  blocking collectives: 101 us -> 37.6 us
  matrix products: 45 us -> 0 us
  Pallas kernels: 0 us -> 25.8 us
  other arithmetic: 25.8 us -> 2.72 us
  waiting for transfers between devices: 31 us -> 10.3 us
  starting transfers between devices: 7.24 us -> 10.8 us
    all_gather x1 -> x0, blocking collectives: 74 us -> none  [per_device(): value_table = lax.all_gather(value_rows, ('aa', 'ba'), axis=0, tiled=True)]
    gather x2 -> x0, local copies, waits for them, and re-layouts: 51.6 us -> none  [blend(): picked = jnp.take(value_table, flat_rows, axis=0)]
    all_to_all x2 -> x0, waiting for transfers between devices: 31 us -> none  [the longest x1 16.7 us: per_device(): lax.all_to_all(stacked, 'ba', split_axis=3, concat_axis=1, tiled=True)]
    dot_general x44 -> x0, matrix products: 26.5 us -> none  [the longest x20 13.6 us: attend(): jnp.einsum('hqk,khd->qhd', weights_bf, value_heads, preferred_element_typ...]
    pallas_call x0 -> x2, Pallas kernels: none -> 25.8 us  [the longest x1 19.9 us: fast_device(): pl.pallas_call(functools.partial(row_kernel, piece_count=group_count, tab...]
    unnamed x1 -> x0, other arithmetic: 22.3 us -> none
    sub x20 -> x0, matrix products: 18.5 us -> none  [attend(): weights_bf = jax.nn.softmax(scores, -1).astype(jnp.bfloat16)]
    ppermute x0 -> x8, starting transfers between devices: none -> 10.8 us  [the longest x7 9.2 us: send(): lax.ppermute(array, axes, [(i, i ^ offset) for i in range(device_count)])]
  transfers between devices with their start and end apart: 2 -> 8, of which waited for: 2 -> 3; matrix products, arithmetic and copies ran while one was open for 0% -> 9% of each run, Pallas kernels for 0% -> 0%
where the time goes in v1:
time: 95.6 us; the launch traced here: 95 us
  blocking collectives  37.6 us (39%)
  Pallas kernels  25.8 us (27%)
  starting transfers between devices  10.8 us (11%)
  waiting for transfers between devices  10.3 us (11%)
  local copies, waits for them, and re-layouts  7.69 us (8%)
  other arithmetic  2.72 us (3%)
    pallas_call x1, Pallas kernels, fast_device(): pl.pallas_call(functools.partial(row_kernel, piece_count=group_count, tab...  19.9 us
    all_to_all x1, blocking collectives, fast_device(): lax.all_to_all(after_rows.reshape(device_count, kept_rows * column_count,...  19.4 us
    all_to_all x1, blocking collectives, fast_device(): lax.all_to_all(encoded.reshape(band_count, local_rows, column_count, C),...  18.2 us
    ppermute x7, waiting for transfers between devices, send(): lax.ppermute(array, axes, [(i, i ^ offset) for i in range(device_count)])  10.3 us
    ppermute x7, starting transfers between devices, send(): lax.ppermute(array, axes, [(i, i ^ offset) for i in range(device_count)])  9.2 us
    pallas_call x1, Pallas kernels, fast_device(): pl.pallas_call(functools.partial(column_kernel, column_count=column_count...  5.89 us
    unnamed x18, local copies, waits for them, and re-layouts  3.08 us
    dynamic_slice x2, local copies, waits for them, and re-layouts, rows_for(): block = lax.dynamic_slice_in_dim(array, member * kept_rows, kept_rows, 0)  2.4 us
  transfers between devices with their start and end apart: 8, of which 3 were waited for; matrix products, arithmetic and copies ran while one was open for 9% of the time, Pallas kernels for 0%

profile of v1, /device:TPU:0, one launch (start us, length us, event | category | flops | bytes accessed | tf_op | source)
XLA Modules:
  0.0 95.0 jit_solution(12440872325884451510)
XLA Ops:
  0.0 4.1 %collective-permute-start.2 = (bf16[48,256]{1,0:T(8,128)(2,1)}, bf16[48,256]{1,0:T(8,128)(2,1)S(1)}, u32[]{:S(2)}, u32[]{:S(2)}) collective-permute-start(bf16[48,256]{1,0:T(8,128)(2,1)} %param.16), channel_id=1, source_target_pairs={{0,16},{1,17},{2,18},{3,19},{4,20},{5,21},{6,22},{7,23},{8,24},{9,... | collective-permute-start | bytes 73736 | tf_op jit(solution)/shard_map/ppermute | solution.py:355
  4.1 1.6 %collective-permute-start.1 = (bf16[48,256]{1,0:T(8,128)(2,1)}, bf16[48,256]{1,0:T(8,128)(2,1)S(1)}, u32[]{:S(2)}, u32[]{:S(2)}) collective-permute-start(bf16[48,256]{1,0:T(8,128)(2,1)} %param.16), channel_id=1, source_target_pairs={{0,8},{1,9},{2,10},{3,11},{4,12},{5,13},{6,14},{7,15},{8,0},{9,1},... | collective-permute-start | bytes 73736 | tf_op jit(solution)/shard_map/ppermute | solution.py:355
  5.6 0.8 constant_dynamic-update-slice_fusion.3
  6.5 0.8 convert_element_type.25
  7.2 0.6 constant_dynamic-slice_fusion
  7.9 1.8 %constant_dynamic-slice_fusion.2 = (bf16[2,256,256]{2,1,0:T(8,128)(2,1)S(1)}, bf16[2,256,256]{2,1,0:T(8,128)(2,1)}) fusion(bf16[4,256,256]{2,1,0:T(8,128)(2,1)} %param.15, s32[]{:T(128)S(6)} %select_n.32, s32[]{:T(128)S(6)} %select_n.31), kind=kLoop, calls=%fused_computation.39 | loop fusion | bytes 1048584 | tf_op jit(solution)/shard_map/dynamic_slice | solution.py:333
  9.7 1.8 %collective-permute-done.3 = bf16[48,256]{1,0:T(8,128)(2,1)S(1)} collective-permute-done((bf16[48,256]{1,0:T(8,128)(2,1)}, bf16[48,256]{1,0:T(8,128)(2,1)S(1)}, u32[]{:S(2)}, u32[]{:S(2)}) %collective-permute-start.3) | collective-permute-done | bytes 24608 | tf_op jit(solution)/shard_map/ppermute | solution.py:355
  11.5 1.5 %collective-permute-start.4 = (bf16[192,256]{1,0:T(8,128)(2,1)S(1)}, bf16[192,256]{1,0:T(8,128)(2,1)S(1)}, u32[]{:S(2)}, u32[]{:S(2)}) collective-permute-start(bf16[192,256]{1,0:T(8,128)(2,1)S(1)} %get-tuple-element.9), channel_id=1, source_target_pairs={{0,4},{1,5},{2,6},{3,7},{4,0},{5,1},{6,2},{7,3},{8,12},{9,13},{10,... | collective-permute-start | bytes 294920 | tf_op jit(solution)/shard_map/ppermute | solution.py:355
  13.0 1.6 %collective-permute-start = (bf16[672,256]{1,0:T(8,128)(2,1)S(1)}, bf16[672,256]{1,0:T(8,128)(2,1)S(1)}, u32[]{:S(2)}, u32[]{:S(2)}) collective-permute-start(bf16[672,256]{1,0:T(8,128)(2,1)S(1)} %pad_maximum_fusion), channel_id=1, source_target_pairs={{0,1},{1,0},{2,3},{3,2},{4,5},{5,4},{6,7},{7,6},{8,9},{9,8},{10,11... | collective-permute-start | bytes 1032200 | tf_op jit(solution)/shard_map/ppermute | solution.py:344
  15.1 1.5 %collective-permute-start.5 = (bf16[192,256]{1,0:T(8,128)(2,1)S(1)}, bf16[192,256]{1,0:T(8,128)(2,1)S(1)}, u32[]{:S(2)}, u32[]{:S(2)}) collective-permute-start(bf16[192,256]{1,0:T(8,128)(2,1)S(1)} %get-tuple-element.9), channel_id=1, source_target_pairs={{0,1},{1,0},{2,3},{3,2},{4,5},{5,4},{6,7},{7,6},{8,9},{9,8},{10,11... | collective-permute-start | bytes 294920 | tf_op jit(solution)/shard_map/ppermute | solution.py:355
  16.9 8.3 %collective-permute-done.5 = bf16[192,256]{1,0:T(8,128)(2,1)S(1)} collective-permute-done((bf16[192,256]{1,0:T(8,128)(2,1)S(1)}, bf16[192,256]{1,0:T(8,128)(2,1)S(1)}, u32[]{:S(2)}, u32[]{:S(2)}) %collective-permute-start.5) | collective-permute-done | bytes 98336 | tf_op jit(solution)/shard_map/ppermute | solution.py:355
  25.3 0.7 pad_add_fusion.slot_ref
  25.9 0.7 copy-done.5
  26.6 0.8 copy.16
  27.4 0.6 fusion.1.refs_2_
  28.1 0.6 slice.19
  28.7 0.7 slice.16
  29.4 0.6 fusion.3.refs_3_
  30.1 0.7 copy-done.1
  30.8 19.9 %rows.1 = bf16[16,2,2,16,256]{4,3,2,1,0:T(8,128)(2,1)} custom-call(s32[2]{0:T(128)} %pad_add_fusion.slot_ref, bf16[2,256,256]{2,1,0:T(8,128)(2,1)} %get-tuple-element.6.refs_0_, bf16[2,256,256]{2,1,0:T(8,128)(2,1)} %bitcast.70, s32[2,8,256]{2,1,0:T(8,128)} %fusion.1.refs_2_, s32[2,8,256]{2,1,0:T(8,128)} %fusion.3.refs_3_, ...), custom_call_target="tpu_custom_call" | custom-call | tf_op jit(solution)/shard_map/rows/pallas_call | solution.py:388
  50.7 19.4 %all_to_all.10 = bf16[32,32,256]{2,1,0:T(8,128)(2,1)} all-to-all(bf16[32,32,256]{2,1,0:T(8,128)(2,1)} %bitcast.63), channel_id=1, replica_groups=mesh['aa'=16,'ba'=2] {'aa','ba'}, dimensions={0} | all-to-all | bytes 1048576 | tf_op jit(solution)/shard_map/all_to_all | solution.py:415
  70.2 5.9 %columns.1 = bf16[1024,256]{1,0:T(8,128)(2,1)} custom-call(bf16[1024,256]{1,0:T(8,128)(2,1)} %bitcast.64, bf16[256,768]{1,0:T(8,128)(2,1)} %project_ref.1, bf16[256,256]{1,0:T(8,128)(2,1)} %output_ref.1, bf16[256,512]{1,0:T(8,128)(2,1)} %expand_ref.1, bf16[512,256]{1,0:T(8,128)(2,1)} %reduce_ref.1, f32[256,4]{1,0:T(8,128)} %bitcast.68), custom_call_target="tpu_custom_call" | custom-call | tf_op jit(solution)/shard_map/columns/pallas_call | solution.py:418
  76.0 18.2 %all_to_all.11 = bf16[16,4,16,256]{3,2,1,0:T(8,128)(2,1)S(1)} all-to-all(bf16[16,4,16,256]{3,2,1,0:T(8,128)(2,1)} %bitcast.65), channel_id=1, replica_groups=mesh['aa'=16,'ba'=2] {'aa'}, dimensions={0} | all-to-all | bytes 1048576 | tf_op jit(solution)/shard_map/all_to_all | solution.py:427
  94.2 0.8 copy.17
  (28 shorter events, 0.9 us)
Async XLA Ops:
  0.0 7.2 %copy-start.2 = (bf16[4,256,8,8]{1,3,2,0:T(8,128)(2,1)S(1)}, bf16[4,256,8,8]{1,3,2,0:T(8,128)(2,1)}, u32[]{:S(2)}) copy-start(bf16[4,256,8,8]{1,3,2,0:T(8,128)(2,1)} %param.20) | copy-start | bytes 393220
  0.0 9.7 %collective-permute-start.2 = (bf16[48,256]{1,0:T(8,128)(2,1)}, bf16[48,256]{1,0:T(8,128)(2,1)S(1)}, u32[]{:S(2)}, u32[]{:S(2)}) collective-permute-start(bf16[48,256]{1,0:T(8,128)(2,1)} %param.16), channel_id=1, source_target_pairs={{0,16},{1,17},{2,18},{3,19},{4,20},{5,21},{6,22},{7,23},{8,24},{9,... | collective-permute-start | bytes 73736 | tf_op jit(solution)/shard_map/ppermute | solution.py:355
  4.1 5.6 %collective-permute-start.1 = (bf16[48,256]{1,0:T(8,128)(2,1)}, bf16[48,256]{1,0:T(8,128)(2,1)S(1)}, u32[]{:S(2)}, u32[]{:S(2)}) collective-permute-start(bf16[48,256]{1,0:T(8,128)(2,1)} %param.16), channel_id=1, source_target_pairs={{0,8},{1,9},{2,10},{3,11},{4,12},{5,13},{6,14},{7,15},{8,0},{9,1},... | collective-permute-start | bytes 73736 | tf_op jit(solution)/shard_map/ppermute | solution.py:355
  5.6 5.8 %collective-permute-start.3 = (bf16[48,256]{1,0:T(8,128)(2,1)}, bf16[48,256]{1,0:T(8,128)(2,1)S(1)}, u32[]{:S(2)}, u32[]{:S(2)}) collective-permute-start(bf16[48,256]{1,0:T(8,128)(2,1)} %param.16), channel_id=1, source_target_pairs={{0,24},{1,25},{2,26},{3,27},{4,28},{5,29},{6,30},{7,31},{8,16},{9,... | collective-permute-start | bytes 73736 | tf_op jit(solution)/shard_map/ppermute | solution.py:355
  7.9 1.8 %copy-start.3 = (s32[4,256,8]{1,2,0:T(8,128)S(1)}, s32[4,256,8]{1,2,0:T(8,128)}, u32[]{:S(2)}) copy-start(s32[4,256,8]{1,2,0:T(8,128)} %param.18) | copy-start | bytes 98308
  7.9 1.8 %copy-start.4 = (s32[4,256,8]{1,2,0:T(8,128)S(1)}, s32[4,256,8]{1,2,0:T(8,128)}, u32[]{:S(2)}) copy-start(s32[4,256,8]{1,2,0:T(8,128)} %param.17) | copy-start | bytes 98308
  11.5 5.4 %collective-permute-start.4 = (bf16[192,256]{1,0:T(8,128)(2,1)S(1)}, bf16[192,256]{1,0:T(8,128)(2,1)S(1)}, u32[]{:S(2)}, u32[]{:S(2)}) collective-permute-start(bf16[192,256]{1,0:T(8,128)(2,1)S(1)} %get-tuple-element.9), channel_id=1, source_target_pairs={{0,4},{1,5},{2,6},{3,7},{4,0},{5,1},{6,2},{7,3},{8,12},{9,13},{10,... | collective-permute-start | bytes 294920 | tf_op jit(solution)/shard_map/ppermute | solution.py:355
  13.0 15.0 %collective-permute-start = (bf16[672,256]{1,0:T(8,128)(2,1)S(1)}, bf16[672,256]{1,0:T(8,128)(2,1)S(1)}, u32[]{:S(2)}, u32[]{:S(2)}) collective-permute-start(bf16[672,256]{1,0:T(8,128)(2,1)S(1)} %pad_maximum_fusion), channel_id=1, source_target_pairs={{0,1},{1,0},{2,3},{3,2},{4,5},{5,4},{6,7},{7,6},{8,9},{9,8},{10,11... | collective-permute-start | bytes 1032200 | tf_op jit(solution)/shard_map/ppermute | solution.py:344
  14.6 10.6 %collective-permute-start.6 = (bf16[192,256]{1,0:T(8,128)(2,1)S(1)}, bf16[192,256]{1,0:T(8,128)(2,1)S(1)}, u32[]{:S(2)}, u32[]{:S(2)}) collective-permute-start(bf16[192,256]{1,0:T(8,128)(2,1)S(1)} %get-tuple-element.9), channel_id=1, source_target_pairs={{0,5},{1,4},{2,7},{3,6},{4,1},{5,0},{6,3},{7,2},{8,13},{9,12},{10,... | collective-permute-start | bytes 294920 | tf_op jit(solution)/shard_map/ppermute | solution.py:355
  15.1 10.1 %collective-permute-start.5 = (bf16[192,256]{1,0:T(8,128)(2,1)S(1)}, bf16[192,256]{1,0:T(8,128)(2,1)S(1)}, u32[]{:S(2)}, u32[]{:S(2)}) collective-permute-start(bf16[192,256]{1,0:T(8,128)(2,1)S(1)} %get-tuple-element.9), channel_id=1, source_target_pairs={{0,1},{1,0},{2,3},{3,2},{4,5},{5,4},{6,7},{7,6},{8,9},{9,8},{10,11... | collective-permute-start | bytes 294920 | tf_op jit(solution)/shard_map/ppermute | solution.py:355
  25.2 4.2 %copy-start = (bf16[768,256]{1,0:T(8,128)(2,1)}, bf16[768,256]{1,0:T(8,128)(2,1)S(1)}, u32[]{:S(2)}) copy-start(bf16[768,256]{1,0:T(8,128)(2,1)S(1)} %constant_dynamic-update-slice_fusion.4.refs_6_) | copy-start | bytes 1179652
  25.2 4.9 %collective-permute-start.7 = (bf16[768,256]{1,0:T(8,128)(2,1)S(1)}, bf16[768,256]{1,0:T(8,128)(2,1)S(1)}, u32[]{:S(2)}, u32[]{:S(2)}) collective-permute-start(bf16[768,256]{1,0:T(8,128)(2,1)S(1)} %constant_dynamic-update-slice_fusion.4.refs_6_), channel_id=1, source_target_pairs={{0,2},{1,3},{2,0},{3,1},{4,6},{5,7},{6,4},{7,5},{8,10},{9,11},{10,... | collective-permute-start | bytes 1179656 | tf_op jit(solution)/shard_map/ppermute | solution.py:355
  25.9 0.7 copy-start.5
  30.1 0.7 copy-start.1

commit v2 on v1

--- a/solution.py
+++ b/solution.py
@@ -130,16 +130,54 @@
     return jnp.concatenate([values, jnp.ones((16, values.shape[1]), values.dtype)], 0)
 
 
+def pack_kernel(
+    bev_ref, weight_ref, camera_ref, level_ref, index_ref, sent_ref, own_ref, numbers_scratch, arrived
+):
+    kept = sent_ref.shape[0]
+    width = bev_ref.shape[1]
+    points = weight_ref.shape[1]
+    group = lax.axis_index("ba")
+    small = [
+        pltpu.make_async_copy(ref, numbers_scratch.at[i], arrived.at[i])
+        for i, ref in enumerate((camera_ref, level_ref, index_ref))
+    ]
+    large = []
+    for member, out_ref in ((1 - group, sent_ref), (group, own_ref)):
+        rows = pl.ds(member * kept, kept)
+        count = len(large) + len(small)
+        large += [
+            pltpu.make_async_copy(bev_ref.at[rows], out_ref.at[:, :width], arrived.at[count]),
+            pltpu.make_async_copy(
+                weight_ref.at[rows],
+                out_ref.at[:, width : width + points],
+                arrived.at[count + 1],
+            ),
+        ]
+    for copy in small + large:
+        copy.start()
+    for copy in small:
+        copy.wait()
+    for member, out_ref in ((1 - group, sent_ref), (group, own_ref)):
+        rows = pl.ds(member * kept, kept)
+        numbers = jnp.concatenate(
+            [numbers_scratch[0, rows] * LEVELS + numbers_scratch[1, rows], numbers_scratch[2, rows]],
+            1,
+        )
+        out_ref[:, width + points :] = numbers.astype(jnp.float32).astype(jnp.bfloat16)
+    for copy in large:
+        copy.wait()
+
+
 def row_kernel(
-    slot_ref,
+    own_ref,
+    got_ref,
     *refs,
-    piece_count,
     table_count,
+    width,
+    map_cells,
+    feature_rows,
+    place_bits,
 ):
-    bev_refs = refs[:piece_count]
-    spot_refs = refs[piece_count : 2 * piece_count]
-    weight_refs = refs[2 * piece_count : 3 * piece_count]
-    refs = refs[3 * piece_count :]
     table_refs = refs[:table_count]
     (
         value_weight_ref,
@@ -148,60 +186,116 @@
         output_ref,
         gains_ref,
         out_ref,
-        table_scratch,
+        score_scratch,
     ) = refs[table_count:]
-
-    @pl.when(pl.program_id(0) == 0)
-    def _():
-        start = 0
-        for table_ref in table_refs:
-            rows = table_ref.shape[0]
-            table_scratch[:, start : start + rows] = lax.dot_general(
+    kept = got_ref.shape[0]
+    points = HEADS * SAMPLES
+    group = lax.axis_index("ba")
+    me = lax.axis_index("aa") * lax.axis_size("ba") + group
+    gains = jnp.concatenate([gains_ref[...], gains_ref[...]], 0).T
+    table = jnp.concatenate(
+        [
+            lax.dot_general(
                 value_weight_ref[...],
                 table_ref[...],
                 (((0,), (1,)), ((), ())),
                 preferred_element_type=jnp.float32,
             ).astype(jnp.bfloat16)
-            start += rows
-
-    width = bev_refs[0].shape[1]
-    cells = piece_count * width
-    table = table_scratch[...]
+            for table_ref in table_refs
+        ],
+        1,
+    )
     entries = table.shape[1]
-    spots = jnp.concatenate([ref[0] for ref in spot_refs], -1)
-    weights = jnp.concatenate([ref[0] for ref in weight_refs], -1).astype(jnp.float32)
+    cells = 2 * width
     line = lax.broadcasted_iota(jnp.int32, (entries, cells), 0)
-    sampled = [None] * HEADS
-    for s in range(SAMPLES):
+
+    def spots_of(maps, numbers):
+        flat = maps * map_cells + numbers
+        owner = jnp.floor((flat.astype(jnp.float32) + 0.5) * (1.0 / feature_rows))
+        owner = owner.astype(jnp.int32)
+        offset = owner ^ me
+        place = jnp.zeros_like(offset)
+        for bit, to in enumerate(place_bits):
+            place = place + ((offset >> bit) & 1) * to
+        return place * feature_rows + (flat - owner * feature_rows)
+
+    def gather_row(r):
+        spots = []
+        for ref in (own_ref, got_ref):
+            numbers = ref[r, width + points :].astype(jnp.float32).astype(jnp.int32)
+            spots.append(spots_of(numbers[:SAMPLES], numbers[SAMPLES:]))
+        weights = [ref[r, width : width + points] for ref in (own_ref, got_ref)]
+        bev = [ref[r, :width] for ref in (own_ref, got_ref)]
+        return (
+            jnp.concatenate(spots, -1),
+            jnp.concatenate(weights, -1).astype(jnp.float32),
+            jnp.concatenate(bev, 0).astype(jnp.float32).T,
+        )
+
+    def sample(sampled, state, s):
+        spots, weights, _ = state
         chosen = jnp.where(line == spots[s : s + 1, :], 1.0, 0.0).astype(jnp.bfloat16)
         picked = jnp.dot(table, chosen, preferred_element_type=jnp.float32)
         for h in range(HEADS):
             row = h * SAMPLES + s
             term = picked[h * HEAD : (h + 1) * HEAD] * weights[row : row + 1, :]
             sampled[h] = term if s == 0 else sampled[h] + term
-    sampled = jnp.concatenate([part.astype(jnp.bfloat16) for part in sampled], 0)
-    bev = jnp.concatenate([ref[0].astype(jnp.float32).T for ref in bev_refs], -1)
-    after_cross = norm_columns(
-        bev + project(cross_ref[...], sampled), gains_ref[:, 0:1]
-    ).astype(jnp.bfloat16)
-    projected = project(project_ref[...], after_cross)
-    query = (projected[:C] * SCALE).astype(jnp.bfloat16)
-    keys = projected[C : 2 * C].astype(jnp.bfloat16)
-    values = projected[2 * C :].astype(jnp.bfloat16)
-    mixed = []
-    for h in range(HEADS):
+
+    def cross(sampled, state):
+        sampled = jnp.concatenate([part.astype(jnp.bfloat16) for part in sampled], 0)
+        after_cross = norm_columns(
+            state[2] + project(cross_ref[...], sampled), gains[:, 0:1]
+        ).astype(jnp.bfloat16)
+        projected = project(project_ref[...], after_cross)
+        query = (projected[:C] * SCALE).astype(jnp.bfloat16)
+        return after_cross, query, projected[C:].astype(jnp.bfloat16)
+
+    def score(parts, h, slot):
+        _, query, rest = parts
         span = slice(h * HEAD, (h + 1) * HEAD)
-        scores = project(keys[span], query[span])
-        powers = jnp.exp2(scores - jnp.max(scores, 0, keepdims=True)).astype(jnp.bfloat16)
-        product = jnp.dot(with_ones(values[span]), powers, preferred_element_type=jnp.float32)
-        mixed.append((product[:HEAD] / product[HEAD : HEAD + 1]).astype(jnp.bfloat16))
-    mixed = jnp.concatenate(mixed, 0)
-    summed = after_cross.astype(jnp.float32) + project(output_ref[...], mixed)
-    after_rows = norm_columns(summed, gains_ref[:, 1:2])
-    for piece in range(piece_count):
-        part = after_rows[:, piece * width : (piece + 1) * width].T.astype(jnp.bfloat16)
-        blocks = part.reshape(out_ref.shape[0], out_ref.shape[3], C)
-        out_ref[:, pl.ds(slot_ref[piece], 1), 0] = blocks[:, None]
+        score_scratch[slot] = project(rest[span], query[span])
+
+    def mix(parts, h, slot):
+        values = parts[2][C + h * HEAD : C + (h + 1) * HEAD]
+        mixed = []
+        for start in range(0, cells, 2 * LANES):
+            scores = score_scratch[slot, :, start : start + 2 * LANES]
+            powers = jnp.exp2(scores - jnp.max(scores, 0, keepdims=True))
+            product = jnp.dot(
+                with_ones(values), powers.astype(jnp.bfloat16), preferred_element_type=jnp.float32
+            )
+            mixed.append((product[:HEAD] / product[HEAD : HEAD + 1]).astype(jnp.bfloat16))
+        return jnp.concatenate(mixed, 1)
+
+    def finish(parts, mixed, r):
+        summed = parts[0].astype(jnp.float32) + project(
+            output_ref[...], jnp.concatenate(mixed, 0)
+        )
+        after_rows = norm_columns(summed, gains[:, 1:2])
+        for piece in range(2):
+            part = after_rows[:, piece * width : (piece + 1) * width].T.astype(jnp.bfloat16)
+            blocks = part.reshape(out_ref.shape[0], out_ref.shape[3], C)
+            slot = group if piece == 0 else 1 - group
+            out_ref[:, pl.ds(slot, 1), r] = blocks[:, None]
+
+    state = gather_row(0)
+    sampled = [None] * HEADS
+    for s in range(SAMPLES):
+        sample(sampled, state, s)
+    for r in range(kept):
+        parts = cross(sampled, state)
+        if r + 1 < kept:
+            state = gather_row(r + 1)
+            sampled = [None] * HEADS
+        score(parts, 0, 0)
+        mixed = []
+        for h in range(HEADS):
+            if h + 1 < HEADS:
+                score(parts, h + 1, (h + 1) % 2)
+            if r + 1 < kept:
+                sample(sampled, state, h)
+            mixed.append(mix(parts, h, h % 2))
+        finish(parts, mixed, r)
 
 
 def column_kernel(
@@ -239,6 +333,7 @@
     query = (projected[:C] * SCALE).astype(jnp.bfloat16)
     keys = projected[C : 2 * C].astype(jnp.bfloat16)
     values = projected[2 * C :].astype(jnp.bfloat16)
+    gains = jnp.concatenate([gains_ref[...], gains_ref[...]], 0).T
     group = max(1, LANES // rows)
     span = group * rows
     owner = lax.broadcasted_iota(jnp.int32, (rows, span), 1) // rows
@@ -269,11 +364,11 @@
         [jnp.concatenate(mixed[h * count : (h + 1) * count], 1) for h in range(HEADS)], 0
     )
     after_columns = norm_columns(
-        cells + project(output_ref[...], mixed), gains_ref[:, 2:3]
+        cells + project(output_ref[...], mixed), gains[:, 2:3]
     ).astype(jnp.bfloat16)
     hidden = jnp.maximum(project(expand_ref[...], after_columns), 0.0).astype(jnp.bfloat16)
     summed = after_columns.astype(jnp.float32) + project(reduce_ref[...], hidden)
-    encoded = norm_columns(summed, gains_ref[:, 3:4]).T
+    encoded = norm_columns(summed, gains[:, 3:4]).T
     for tile, start in enumerate(tiles):
         for column in range(column_count):
             cells_scratch[tile, pl.ds(column, rows, stride=column_count), :] = encoded[
@@ -315,102 +410,77 @@
     group_count = lax.axis_size("ba")
     device_count = band_count * group_count
     axes = ("aa", "ba")
-    group = lax.axis_index("ba")
-    me = lax.axis_index("aa") * group_count + group
     feature_rows = features.shape[0]
     map_cells = feature_rows * device_count // (CAMS * LEVELS)
     local_rows, width = bev_query.shape[:2]
     kept_rows = local_rows // group_count
     column_count = width // band_count
 
-    maps = jnp.swapaxes(camera_ids * LEVELS + level_ids, 1, 2).astype(jnp.bfloat16)
-    cells = jnp.swapaxes(sample_index, 1, 2).astype(jnp.bfloat16)
-    weights = sample_weight.transpose(0, 2, 3, 1).reshape(local_rows, HEADS * SAMPLES, width)
-
-    def rows_for(member):
-        parts = []
-        for array in (bev_query, weights, maps, cells):
-            block = lax.dynamic_slice_in_dim(array, member * kept_rows, kept_rows, 0)
-            parts.append(block)
-        return parts
-
-    def pack(parts):
-        return jnp.concatenate([part.reshape(-1, C) for part in parts], 0)
-
-    own_parts = rows_for(group)
-    pieces = [own_parts]
-    for offset in range(1, group_count):
-        sent = pack(rows_for(group ^ offset))
-        got = lax.ppermute(sent, "ba", [(i, i ^ offset) for i in range(group_count)])
-        parts, start = [], 0
-        for part in own_parts:
-            rows = part.size // C
-            parts.append(got[start : start + rows].reshape(part.shape))
-            start += rows
-        pieces.append(parts)
+    whole = pl.BlockSpec(memory_space=pltpu.VMEM)
+    params = pltpu.CompilerParams(vmem_limit_bytes=24 * 1024 * 1024)
+
+    packed = jax.ShapeDtypeStruct((kept_rows, width + (HEADS + 2) * SAMPLES, C), jnp.bfloat16)
+    sent, own = pl.pallas_call(
+        pack_kernel,
+        out_shape=(packed, packed),
+        in_specs=[pl.BlockSpec(memory_space=pltpu.HBM)] * 5,
+        out_specs=(whole, whole),
+        scratch_shapes=[
+            pltpu.VMEM((3, local_rows, SAMPLES, width), jnp.int32),
+            pltpu.SemaphoreType.DMA((7,)),
+        ],
+        compiler_params=pltpu.CompilerParams(vmem_limit_bytes=58 * 1024 * 1024),
+        name="pack",
+    )(
+        bev_query,
+        sample_weight.transpose(0, 2, 3, 1).reshape(local_rows, HEADS * SAMPLES, width),
+        jnp.swapaxes(camera_ids, 1, 2),
+        jnp.swapaxes(level_ids, 1, 2),
+        jnp.swapaxes(sample_index, 1, 2),
+    )
+    got = lax.ppermute(sent, "ba", [(0, 1), (1, 0)])
 
     stages = exchange_order(band_count, group_count)
 
     def send(array, offset):
         return lax.ppermute(array, axes, [(i, i ^ offset) for i in range(device_count)])
 
-    held = features
-    for offsets in stages[:2]:
-        held = jnp.concatenate([held] + [send(held, offset) for offset in offsets[1:]], 0)
-    tables = [held] + [send(held, offset) for offset in stages[2][1:]]
+    held = jnp.concatenate([features] + [send(features, offset) for offset in stages[0][1:]], 0)
+    tables = [held] + [send(held, offset) for offset in stages[1][1:]]
+    tables = tables + [send(table, stages[2][1]) for table in tables]
 
     order = [0]
     for offsets in stages:
         order = [base ^ offset for offset in offsets for base in order]
-    place_of = [0] * device_count
-    for place, offset in enumerate(order):
-        place_of[offset] = place
-
-    def spots_of(parts):
-        flat = parts[2].astype(jnp.int32) * map_cells + parts[3].astype(jnp.int32)
-        offset = (flat // feature_rows) ^ me
-        place = jnp.zeros_like(offset)
-        for bit in range(device_count.bit_length() - 1):
-            place = place + ((offset >> bit) & 1) * place_of[1 << bit]
-        return place * feature_rows + flat % feature_rows
-
-    slots = jnp.stack([group ^ offset for offset in range(group_count)]).astype(jnp.int32)
-    gains = norm_gains.T
-    whole = pl.BlockSpec(memory_space=pltpu.VMEM)
-
-    def per_row(array):
-        return pl.BlockSpec((1,) + array.shape[1:], lambda i: (i, 0, 0))
-
-    bev_pieces = [parts[0] for parts in pieces]
-    spot_pieces = [spots_of(parts) for parts in pieces]
-    weight_pieces = [parts[1] for parts in pieces]
+    place_bits = tuple(
+        order.index(1 << bit) for bit in range(device_count.bit_length() - 1)
+    )
+
     sent_shape = (band_count, group_count, kept_rows, column_count, C)
     after_rows = pl.pallas_call(
         functools.partial(
-            row_kernel, piece_count=group_count, table_count=len(tables)
+            row_kernel,
+            table_count=len(tables),
+            width=width,
+            map_cells=map_cells,
+            feature_rows=feature_rows,
+            place_bits=place_bits,
         ),
         out_shape=jax.ShapeDtypeStruct(sent_shape, jnp.bfloat16),
-        grid=(kept_rows,),
-        in_specs=[pl.BlockSpec(memory_space=pltpu.SMEM)]
-        + [per_row(array) for array in bev_pieces + spot_pieces + weight_pieces]
-        + [whole] * (len(tables) + 5),
-        out_specs=pl.BlockSpec(
-            (band_count, group_count, 1, column_count, C), lambda i: (0, 0, i, 0, 0)
-        ),
-        scratch_shapes=[pltpu.VMEM((C, feature_rows * device_count), jnp.bfloat16)],
-        compiler_params=pltpu.CompilerParams(vmem_limit_bytes=56 * 1024 * 1024),
+        in_specs=[whole] * (len(tables) + 7),
+        out_specs=whole,
+        scratch_shapes=[pltpu.VMEM((2, 2 * width, 2 * width), jnp.float32)],
+        compiler_params=params,
         name="rows",
     )(
-        slots,
-        *bev_pieces,
-        *spot_pieces,
-        *weight_pieces,
+        own,
+        got,
         *tables,
         value_weight,
         cross_weight,
         row_project,
         row_output,
-        gains,
+        norm_gains,
     )
     lines = lax.all_to_all(
         after_rows.reshape(device_count, kept_rows * column_count, C), axes, 0, 0, tiled=True
@@ -421,9 +491,9 @@
         in_specs=[whole] * 6,
         out_specs=whole,
         scratch_shapes=[pltpu.VMEM((C // LANES, lines.shape[0], LANES), jnp.float32)],
-        compiler_params=pltpu.CompilerParams(vmem_limit_bytes=56 * 1024 * 1024),
+        compiler_params=params,
         name="columns",
-    )(lines, column_project, column_output, expand_weight, reduce_weight, gains)
+    )(lines, column_project, column_output, expand_weight, reduce_weight, norm_gains)
     returned = lax.all_to_all(
         encoded.reshape(band_count, local_rows, column_count, C), "aa", 0, 0, tiled=True
     )
@@ -436,9 +506,9 @@
     local_rows, width = rows // band_count, columns // group_count
     return (
         band_count in (8, 16)
-        and group_count in (2, 4)
+        and group_count == 2
         and local_rows % group_count == 0
-        and width % C == 0
+        and width == C
         and width % (16 * band_count) == 0
         and rows in (32, 64, 128)
     )

time: 95.6 us -> 82.1 us (0.86)
  local copies, waits for them, and re-layouts: 7.69 us -> 1.87 us
  Pallas kernels: 25.8 us -> 20.5 us
  other arithmetic: 2.72 us -> 0 us
  waiting for transfers between devices: 10.3 us -> 9.34 us
    pallas_call x1 -> x2, Pallas kernels: 19.9 us -> 16.9 us  [the longest x1 14.8 us: fast_device(): pl.pallas_call(functools.partial(row_kernel, table_count=len(tables), wid...]
    dynamic_slice x2 -> x0, local copies, waits for them, and re-layouts: 2.4 us -> none  [rows_for(): block = lax.dynamic_slice_in_dim(array, member * kept_rows, kept_rows, 0)]
    pallas_call x1, Pallas kernels: 5.89 us -> 3.67 us  [fast_device(): pl.pallas_call(functools.partial(column_kernel, column_count=column_count...]
    unnamed x18 -> x25, local copies, waits for them, and re-layouts: 3.08 us -> 1.03 us
    slice x2 -> x0, local copies, waits for them, and re-layouts: 1.36 us -> none  [fast_device(): parts.append(got[start:start + rows].reshape(part.shape))]
    add x2 -> x0, other arithmetic: 1.27 us -> none  [spots_of(): return place * feature_rows + flat % feature_rows]
    all_to_all x1, blocking collectives: 19.4 us -> 20.6 us  [fast_device(): lax.all_to_all(after_rows.reshape(device_count, kept_rows * column_count,...]
    ppermute x7 -> x10, waiting for transfers between devices: 10.3 us -> 9.34 us  [send(): lax.ppermute(array, axes, [(i, i ^ offset) for i in range(device_count)])]
  transfers between devices with their start and end apart: 8 -> 11, of which waited for: 3 -> 5; matrix products, arithmetic and copies ran while one was open for 9% -> 0% of each run, Pallas kernels for 0% -> 3%
where the time goes in v2:
time: 82.1 us; the launch traced here: 81.9 us
  blocking collectives  38.5 us (47%)
  Pallas kernels  20.5 us (25%)
  starting transfers between devices  11.4 us (14%)
  waiting for transfers between devices  9.34 us (11%)
  local copies, waits for them, and re-layouts  1.87 us (2%)
    all_to_all x1, blocking collectives, fast_device(): lax.all_to_all(after_rows.reshape(device_count, kept_rows * column_count,...  20.6 us
    all_to_all x1, blocking collectives, fast_device(): lax.all_to_all(encoded.reshape(band_count, local_rows, column_count, C),...  18 us
    pallas_call x1, Pallas kernels, fast_device(): pl.pallas_call(functools.partial(row_kernel, table_count=len(tables), wid...  14.8 us
    ppermute x10, starting transfers between devices, send(): lax.ppermute(array, axes, [(i, i ^ offset) for i in range(device_count)])  9.65 us
    ppermute x10, waiting for transfers between devices, send(): lax.ppermute(array, axes, [(i, i ^ offset) for i in range(device_count)])  9.34 us
    pallas_call x1, Pallas kernels, fast_device(): pl.pallas_call(functools.partial(column_kernel, column_count=column_count...  3.67 us
    pallas_call x1, Pallas kernels, fast_device(): pl.pallas_call(pack_kernel, out_shape=(packed, packed), in_specs=[pl.Bloc...  2.08 us
    ppermute x1, starting transfers between devices, fast_device(): got = lax.ppermute(sent, 'ba', [(0, 1), (1, 0)])  1.8 us
  transfers between devices with their start and end apart: 11, of which 5 were waited for; matrix products, arithmetic and copies ran while one was open for 0% of the time, Pallas kernels for 3%

profile of v2, /device:TPU:0, one launch (start us, length us, event | category | flops | bytes accessed | tf_op | source)
XLA Modules:
  0.0 81.9 jit_solution(1941952670187193866)
XLA Ops:
  0.0 4.1 %collective-permute-start.2 = (bf16[48,256]{1,0:T(8,128)(2,1)}, bf16[48,256]{1,0:T(8,128)(2,1)S(1)}, u32[]{:S(2)}, u32[]{:S(2)}) collective-permute-start(bf16[48,256]{1,0:T(8,128)(2,1)} %param.16), channel_id=1, source_target_pairs={{0,16},{1,17},{2,18},{3,19},{4,20},{5,21},{6,22},{7,23},{8,24},{9,... | collective-permute-start | bytes 73736 | tf_op jit(solution)/shard_map/ppermute | solution.py:446
  4.1 1.6 %collective-permute-start.1 = (bf16[48,256]{1,0:T(8,128)(2,1)}, bf16[48,256]{1,0:T(8,128)(2,1)S(1)}, u32[]{:S(2)}, u32[]{:S(2)}) collective-permute-start(bf16[48,256]{1,0:T(8,128)(2,1)} %param.16), channel_id=1, source_target_pairs={{0,8},{1,9},{2,10},{3,11},{4,12},{5,13},{6,14},{7,15},{8,0},{9,1},... | collective-permute-start | bytes 73736 | tf_op jit(solution)/shard_map/ppermute | solution.py:446
  5.7 2.1 %pack.1 = (bf16[2,336,256]{2,1,0:T(8,128)(2,1)}, bf16[2,336,256]{2,1,0:T(8,128)(2,1)}) custom-call(bf16[4,256,256]{2,1,0:T(8,128)(2,1)} %bev_ref.1, bf16[4,64,256]{2,1,0:T(8,128)(2,1)} %bitcast.15, s32[4,8,256]{2,1,0:T(8,128)} %bitcast.16, s32[4,8,256]{2,1,0:T(8,128)} %bitcast.17, s32[4,8,256]{2,1,0:T(8,128)} %bitcast.18), custom_call_target="tpu_custom_call" | custom-call | tf_op jit(solution)/shard_map/pack/pallas_call | solution.py:423
  7.8 0.0 copy-start.5
  7.8 1.8 %collective-permute-start = (bf16[2,336,256]{2,1,0:T(8,128)(2,1)}, bf16[2,336,256]{2,1,0:T(8,128)(2,1)S(1)}, u32[]{:S(2)}, u32[]{:S(2)}) collective-permute-start(bf16[2,336,256]{2,1,0:T(8,128)(2,1)} %get-tuple-element.8), channel_id=1, source_target_pairs={{0,1},{1,0},{2,3},{3,2},{4,5},{5,4},{6,7},{7,6},{8,9},{9,8},{10,11... | collective-permute-start | bytes 1032200 | tf_op jit(solution)/shard_map/ppermute | solution.py:441
  9.6 1.9 %collective-permute-done.3 = bf16[48,256]{1,0:T(8,128)(2,1)S(1)} collective-permute-done((bf16[48,256]{1,0:T(8,128)(2,1)}, bf16[48,256]{1,0:T(8,128)(2,1)S(1)}, u32[]{:S(2)}, u32[]{:S(2)}) %collective-permute-start.3) | collective-permute-done | bytes 24608 | tf_op jit(solution)/shard_map/ppermute | solution.py:446
  11.5 2.4 %collective-permute-start.6 = (bf16[192,256]{1,0:T(8,128)(2,1)S(1)}, bf16[192,256]{1,0:T(8,128)(2,1)S(1)}, u32[]{:S(2)}, u32[]{:S(2)}) collective-permute-start(bf16[192,256]{1,0:T(8,128)(2,1)S(1)} %constant_dynamic-update-slice_fusion.refs_0_), channel_id=1, source_target_pairs={{0,5},{1,4},{2,7},{3,6},{4,1},{5,0},{6,3},{7,2},{8,13},{9,12},{10,... | collective-permute-start | bytes 294920 | tf_op jit(solution)/shard_map/ppermute | solution.py:446
  13.9 0.5 collective-permute-start.5
  14.4 0.5 collective-permute-start.4
  15.0 2.8 %collective-permute-done.6.refs_3_ = bf16[192,256]{1,0:T(8,128)(2,1)S(1)} collective-permute-done((bf16[192,256]{1,0:T(8,128)(2,1)S(1)}, bf16[192,256]{1,0:T(8,128)(2,1)S(1)}, u32[]{:S(2)}, u32[]{:S(2)}) %collective-permute-start.6) | collective-permute-done | bytes 98336 | tf_op jit(solution)/shard_map/ppermute | solution.py:446
  17.8 3.7 %collective-permute-done.5.refs_2_ = bf16[192,256]{1,0:T(8,128)(2,1)S(1)} collective-permute-done((bf16[192,256]{1,0:T(8,128)(2,1)S(1)}, bf16[192,256]{1,0:T(8,128)(2,1)S(1)}, u32[]{:S(2)}, u32[]{:S(2)}) %collective-permute-start.5) | collective-permute-done | bytes 98336 | tf_op jit(solution)/shard_map/ppermute | solution.py:446
  21.5 0.5 collective-permute-start.8
  22.0 0.8 collective-permute-done.9.refs_6_
  22.8 0.2 collective-permute-done.8.refs_5_
  23.0 1.0 %copy-done.2 = bf16[2,336,256]{2,1,0:T(8,128)(2,1)S(1)} copy-done((bf16[2,336,256]{2,1,0:T(8,128)(2,1)S(1)}, bf16[2,336,256]{2,1,0:T(8,128)(2,1)}, u32[]{:S(2)}) %copy-start.2) | copy-done | bytes 344088
  24.0 14.8 %rows.1 = bf16[16,2,2,16,256]{4,3,2,1,0:T(8,128)(2,1)S(1)} custom-call(bf16[2,336,256]{2,1,0:T(8,128)(2,1)S(1)} %copy-done.2, bf16[2,336,256]{2,1,0:T(8,128)(2,1)S(1)} %collective-permute-done.got_ref, bf16[192,256]{1,0:T(8,128)(2,1)S(1)} %constant_dynamic-update-slice_fusion.refs_0_, bf16[192,256]{1,0:T(8,128)(2,1)S(1)} %collective-permute-done.4.refs_1_, ...), custom_call_target="tpu_custom_call" | custom-call | tf_op jit(solution)/shard_map/rows/pallas_call | solution.py:460
  38.8 0.0 copy-start
  38.8 0.0 copy-start.3
  38.8 0.0 copy-start.4
  38.8 0.0 copy-start.8
  38.8 20.6 %all_to_all.10 = bf16[32,32,256]{2,1,0:T(8,128)(2,1)S(1)} all-to-all(bf16[32,32,256]{2,1,0:T(8,128)(2,1)S(1)} %bitcast.11), channel_id=1, replica_groups=mesh['aa'=16,'ba'=2] {'aa','ba'}, dimensions={0} | all-to-all | bytes 1048576 | tf_op jit(solution)/shard_map/all_to_all | solution.py:485
  59.4 3.7 %columns.1 = bf16[1024,256]{1,0:T(8,128)(2,1)S(1)} custom-call(bf16[1024,256]{1,0:T(8,128)(2,1)S(1)} %bitcast.12, bf16[256,768]{1,0:T(8,128)(2,1)S(1)} %copy-done, bf16[256,256]{1,0:T(8,128)(2,1)S(1)} %copy-done.8, bf16[256,512]{1,0:T(8,128)(2,1)S(1)} %copy-done.3, bf16[512,256]{1,0:T(8,128)(2,1)S(1)} %copy-done.4, f32[4,256]{1,0:T(4,128)S(1)} %copy-done.9), custom_call_target="tpu_custom_call" | custom-call | tf_op jit(solution)/shard_map/columns/pallas_call | solution.py:488
  63.1 18.0 %all_to_all.11 = bf16[16,4,16,256]{3,2,1,0:T(8,128)(2,1)S(1)} all-to-all(bf16[16,4,16,256]{3,2,1,0:T(8,128)(2,1)S(1)} %bitcast.13), channel_id=1, replica_groups=mesh['aa'=16,'ba'=2] {'aa'}, dimensions={0} | all-to-all | bytes 1048576 | tf_op jit(solution)/shard_map/all_to_all | solution.py:497
  81.0 0.8 %copy.16 = bf16[4,16,16,256]{3,2,1,0:T(8,128)(2,1)} copy(bf16[4,16,16,256]{3,2,0,1:T(8,128)(2,1)S(1)} %bitcast.14) | data formatting | bytes 1048576 | tf_op jit(solution)/shard_map/transpose | solution.py:500
  (30 shorter events, 0.1 us)
Async XLA Ops:
  0.0 9.6 %collective-permute-start.2 = (bf16[48,256]{1,0:T(8,128)(2,1)}, bf16[48,256]{1,0:T(8,128)(2,1)S(1)}, u32[]{:S(2)}, u32[]{:S(2)}) collective-permute-start(bf16[48,256]{1,0:T(8,128)(2,1)} %param.16), channel_id=1, source_target_pairs={{0,16},{1,17},{2,18},{3,19},{4,20},{5,21},{6,22},{7,23},{8,24},{9,... | collective-permute-start | bytes 73736 | tf_op jit(solution)/shard_map/ppermute | solution.py:446
  4.1 5.5 %collective-permute-start.1 = (bf16[48,256]{1,0:T(8,128)(2,1)}, bf16[48,256]{1,0:T(8,128)(2,1)S(1)}, u32[]{:S(2)}, u32[]{:S(2)}) collective-permute-start(bf16[48,256]{1,0:T(8,128)(2,1)} %param.16), channel_id=1, source_target_pairs={{0,8},{1,9},{2,10},{3,11},{4,12},{5,13},{6,14},{7,15},{8,0},{9,1},... | collective-permute-start | bytes 73736 | tf_op jit(solution)/shard_map/ppermute | solution.py:446
  5.6 5.8 %collective-permute-start.3 = (bf16[48,256]{1,0:T(8,128)(2,1)}, bf16[48,256]{1,0:T(8,128)(2,1)S(1)}, u32[]{:S(2)}, u32[]{:S(2)}) collective-permute-start(bf16[48,256]{1,0:T(8,128)(2,1)} %param.16), channel_id=1, source_target_pairs={{0,24},{1,25},{2,26},{3,27},{4,28},{5,29},{6,30},{7,31},{8,16},{9,... | collective-permute-start | bytes 73736 | tf_op jit(solution)/shard_map/ppermute | solution.py:446
  5.6 3.9 %copy-start.10 = (bf16[48,256]{1,0:T(8,128)(2,1)S(1)}, bf16[48,256]{1,0:T(8,128)(2,1)}, u32[]{:S(2)}) copy-start(bf16[48,256]{1,0:T(8,128)(2,1)} %param.16) | copy-start | bytes 73732
  5.6 17.3 %copy-start.1 = (bf16[256,768]{1,0:T(8,128)(2,1)S(1)}, bf16[256,768]{1,0:T(8,128)(2,1)}, u32[]{:S(2)}) copy-start(bf16[256,768]{1,0:T(8,128)(2,1)} %refs_10_.1) | copy-start | bytes 1179652
  5.7 17.3 %copy-start.6 = (bf16[256,256]{1,0:T(8,128)(2,1)S(1)}, bf16[256,256]{1,0:T(8,128)(2,1)}, u32[]{:S(2)}) copy-start(bf16[256,256]{1,0:T(8,128)(2,1)} %refs_9_.1) | copy-start | bytes 393220
  5.7 17.3 %copy-start.7 = (bf16[256,256]{1,0:T(8,128)(2,1)S(1)}, bf16[256,256]{1,0:T(8,128)(2,1)}, u32[]{:S(2)}) copy-start(bf16[256,256]{1,0:T(8,128)(2,1)} %refs_11_.1) | copy-start | bytes 393220
  7.8 15.2 %copy-start.5 = (bf16[256,256]{1,0:T(8,128)(2,1)S(1)}, bf16[256,256]{1,0:T(8,128)(2,1)}, u32[]{:S(2)}) copy-start(bf16[256,256]{1,0:T(8,128)(2,1)} %refs_8_.1) | copy-start | bytes 393220
  7.8 15.2 %collective-permute-start = (bf16[2,336,256]{2,1,0:T(8,128)(2,1)}, bf16[2,336,256]{2,1,0:T(8,128)(2,1)S(1)}, u32[]{:S(2)}, u32[]{:S(2)}) collective-permute-start(bf16[2,336,256]{2,1,0:T(8,128)(2,1)} %get-tuple-element.8), channel_id=1, source_target_pairs={{0,1},{1,0},{2,3},{3,2},{4,5},{5,4},{6,7},{7,6},{8,9},{9,8},{10,11... | collective-permute-start | bytes 1032200 | tf_op jit(solution)/shard_map/ppermute | solution.py:441
  11.5 11.5 %copy-start.9 = (f32[4,256]{1,0:T(4,128)S(1)}, f32[4,256]{1,0:T(4,128)}, u32[]{:S(2)}) copy-start(f32[4,256]{1,0:T(4,128)} %gains_ref.1) | copy-start | bytes 12292
  11.5 6.3 %collective-permute-start.6 = (bf16[192,256]{1,0:T(8,128)(2,1)S(1)}, bf16[192,256]{1,0:T(8,128)(2,1)S(1)}, u32[]{:S(2)}, u32[]{:S(2)}) collective-permute-start(bf16[192,256]{1,0:T(8,128)(2,1)S(1)} %constant_dynamic-update-slice_fusion.refs_0_), channel_id=1, source_target_pairs={{0,5},{1,4},{2,7},{3,6},{4,1},{5,0},{6,3},{7,2},{8,13},{9,12},{10,... | collective-permute-start | bytes 294920 | tf_op jit(solution)/shard_map/ppermute | solution.py:446
  13.9 7.6 %collective-permute-start.5 = (bf16[192,256]{1,0:T(8,128)(2,1)S(1)}, bf16[192,256]{1,0:T(8,128)(2,1)S(1)}, u32[]{:S(2)}, u32[]{:S(2)}) collective-permute-start(bf16[192,256]{1,0:T(8,128)(2,1)S(1)} %constant_dynamic-update-slice_fusion.refs_0_), channel_id=1, source_target_pairs={{0,1},{1,0},{2,3},{3,2},{4,5},{5,4},{6,7},{7,6},{8,9},{9,8},{10,11... | collective-permute-start | bytes 294920 | tf_op jit(solution)/shard_map/ppermute | solution.py:446
  14.4 7.1 %collective-permute-start.4 = (bf16[192,256]{1,0:T(8,128)(2,1)S(1)}, bf16[192,256]{1,0:T(8,128)(2,1)S(1)}, u32[]{:S(2)}, u32[]{:S(2)}) collective-permute-start(bf16[192,256]{1,0:T(8,128)(2,1)S(1)} %constant_dynamic-update-slice_fusion.refs_0_), channel_id=1, source_target_pairs={{0,4},{1,5},{2,6},{3,7},{4,0},{5,1},{6,2},{7,3},{8,12},{9,13},{10,... | collective-permute-start | bytes 294920 | tf_op jit(solution)/shard_map/ppermute | solution.py:446
  15.0 7.0 %collective-permute-start.7 = (bf16[192,256]{1,0:T(8,128)(2,1)S(1)}, bf16[192,256]{1,0:T(8,128)(2,1)S(1)}, u32[]{:S(2)}, u32[]{:S(2)}) collective-permute-start(bf16[192,256]{1,0:T(8,128)(2,1)S(1)} %constant_dynamic-update-slice_fusion.refs_0_), channel_id=1, source_target_pairs={{0,2},{1,3},{2,0},{3,1},{4,6},{5,7},{6,4},{7,5},{8,10},{9,11},{10,... | collective-permute-start | bytes 294920 | tf_op jit(solution)/shard_map/ppermute | solution.py:446
  17.8 4.2 %collective-permute-start.10 = (bf16[192,256]{1,0:T(8,128)(2,1)S(1)}, bf16[192,256]{1,0:T(8,128)(2,1)S(1)}, u32[]{:S(2)}, u32[]{:S(2)}) collective-permute-start(bf16[192,256]{1,0:T(8,128)(2,1)S(1)} %collective-permute-done.6.refs_3_), channel_id=1, source_target_pairs={{0,2},{1,3},{2,0},{3,1},{4,6},{5,7},{6,4},{7,5},{8,10},{9,11},{10,... | collective-permute-start | bytes 294920 | tf_op jit(solution)/shard_map/ppermute | solution.py:446
  21.5 1.3 %collective-permute-start.9 = (bf16[192,256]{1,0:T(8,128)(2,1)S(1)}, bf16[192,256]{1,0:T(8,128)(2,1)S(1)}, u32[]{:S(2)}, u32[]{:S(2)}) collective-permute-start(bf16[192,256]{1,0:T(8,128)(2,1)S(1)} %collective-permute-done.5.refs_2_), channel_id=1, source_target_pairs={{0,2},{1,3},{2,0},{3,1},{4,6},{5,7},{6,4},{7,5},{8,10},{9,11},{10,... | collective-permute-start | bytes 294920 | tf_op jit(solution)/shard_map/ppermute | solution.py:446
  21.5 1.5 %collective-permute-start.8 = (bf16[192,256]{1,0:T(8,128)(2,1)S(1)}, bf16[192,256]{1,0:T(8,128)(2,1)S(1)}, u32[]{:S(2)}, u32[]{:S(2)}) collective-permute-start(bf16[192,256]{1,0:T(8,128)(2,1)S(1)} %collective-permute-done.4.refs_1_), channel_id=1, source_target_pairs={{0,2},{1,3},{2,0},{3,1},{4,6},{5,7},{6,4},{7,5},{8,10},{9,11},{10,... | collective-permute-start | bytes 294920 | tf_op jit(solution)/shard_map/ppermute | solution.py:446
  23.0 1.0 %copy-start.2 = (bf16[2,336,256]{2,1,0:T(8,128)(2,1)S(1)}, bf16[2,336,256]{2,1,0:T(8,128)(2,1)}, u32[]{:S(2)}) copy-start(bf16[2,336,256]{2,1,0:T(8,128)(2,1)} %get-tuple-element.7.own_ref) | copy-start | bytes 1032196
  38.8 20.6 %copy-start = (bf16[256,768]{1,0:T(8,128)(2,1)S(1)}, bf16[256,768]{1,0:T(8,128)(2,1)}, u32[]{:S(2)}) copy-start(bf16[256,768]{1,0:T(8,128)(2,1)} %project_ref.1) | copy-start | bytes 1179652
  38.8 20.6 %copy-start.3 = (bf16[256,512]{1,0:T(8,128)(2,1)S(1)}, bf16[256,512]{1,0:T(8,128)(2,1)}, u32[]{:S(2)}) copy-start(bf16[256,512]{1,0:T(8,128)(2,1)} %expand_ref.1) | copy-start | bytes 786436
  38.8 20.6 %copy-start.4 = (bf16[512,256]{1,0:T(8,128)(2,1)S(1)}, bf16[512,256]{1,0:T(8,128)(2,1)}, u32[]{:S(2)}) copy-start(bf16[512,256]{1,0:T(8,128)(2,1)} %reduce_ref.1) | copy-start | bytes 786436
  38.8 20.6 %copy-start.8 = (bf16[256,256]{1,0:T(8,128)(2,1)S(1)}, bf16[256,256]{1,0:T(8,128)(2,1)}, u32[]{:S(2)}) copy-start(bf16[256,256]{1,0:T(8,128)(2,1)} %output_ref.1) | copy-start | bytes 393220

commit v3 on v2

--- a/solution.py
+++ b/solution.py
@@ -7,6 +7,7 @@
 from jax.experimental import pallas as pl
 from jax.experimental.pallas import tpu as pltpu
 from jax.sharding import PartitionSpec as P
+
 
 C = 256
 HEADS = 8
@@ -131,68 +132,55 @@
 
 
 def pack_kernel(
-    bev_ref, weight_ref, camera_ref, level_ref, index_ref, sent_ref, own_ref, numbers_scratch, arrived
+    weight_ref, camera_ref, level_ref, index_ref, sent_ref, own_ref, numbers_scratch, arrived
 ):
     kept = sent_ref.shape[0]
-    width = bev_ref.shape[1]
     points = weight_ref.shape[1]
     group = lax.axis_index("ba")
+    members = ((1 - group, sent_ref), (group, own_ref))
     small = [
         pltpu.make_async_copy(ref, numbers_scratch.at[i], arrived.at[i])
         for i, ref in enumerate((camera_ref, level_ref, index_ref))
     ]
-    large = []
-    for member, out_ref in ((1 - group, sent_ref), (group, own_ref)):
-        rows = pl.ds(member * kept, kept)
-        count = len(large) + len(small)
-        large += [
-            pltpu.make_async_copy(bev_ref.at[rows], out_ref.at[:, :width], arrived.at[count]),
-            pltpu.make_async_copy(
-                weight_ref.at[rows],
-                out_ref.at[:, width : width + points],
-                arrived.at[count + 1],
-            ),
-        ]
+    large = [
+        pltpu.make_async_copy(
+            weight_ref.at[pl.ds(member * kept, kept)],
+            out_ref.at[:, :points],
+            arrived.at[len(small) + i],
+        )
+        for i, (member, out_ref) in enumerate(members)
+    ]
     for copy in small + large:
         copy.start()
     for copy in small:
         copy.wait()
-    for member, out_ref in ((1 - group, sent_ref), (group, own_ref)):
+    for member, out_ref in members:
         rows = pl.ds(member * kept, kept)
         numbers = jnp.concatenate(
             [numbers_scratch[0, rows] * LEVELS + numbers_scratch[1, rows], numbers_scratch[2, rows]],
             1,
         )
-        out_ref[:, width + points :] = numbers.astype(jnp.float32).astype(jnp.bfloat16)
+        out_ref[:, points:] = numbers.astype(jnp.float32).astype(jnp.bfloat16)
     for copy in large:
         copy.wait()
 
 
-def row_kernel(
-    own_ref,
-    got_ref,
+def sample_kernel(
+    value_weight_ref,
     *refs,
-    table_count,
-    width,
+    pieces,
+    known,
     map_cells,
     feature_rows,
     place_bits,
 ):
-    table_refs = refs[:table_count]
-    (
-        value_weight_ref,
-        cross_ref,
-        project_ref,
-        output_ref,
-        gains_ref,
-        out_ref,
-        score_scratch,
-    ) = refs[table_count:]
-    kept = got_ref.shape[0]
+    table_refs = refs[: len(pieces)]
+    out_ref = refs[-1]
+    own_ref, *rest = refs[len(pieces) : -1]
+    kept, _, width = own_ref.shape
     points = HEADS * SAMPLES
-    group = lax.axis_index("ba")
-    me = lax.axis_index("aa") * lax.axis_size("ba") + group
-    gains = jnp.concatenate([gains_ref[...], gains_ref[...]], 0).T
+    size = table_refs[0].shape[0]
+    me = lax.axis_index("aa") * lax.axis_size("ba") + lax.axis_index("ba")
     table = jnp.concatenate(
         [
             lax.dot_general(
@@ -205,9 +193,8 @@
         ],
         1,
     )
-    entries = table.shape[1]
-    cells = 2 * width
-    line = lax.broadcasted_iota(jnp.int32, (entries, cells), 0)
+    step = lax.broadcasted_iota(jnp.int32, (size, width), 0)
+    line = jnp.concatenate([(step + piece * size).astype(jnp.int16) for piece in pieces], 0)
 
     def spots_of(maps, numbers):
         flat = maps * map_cells + numbers
@@ -219,32 +206,55 @@
             place = place + ((offset >> bit) & 1) * to
         return place * feature_rows + (flat - owner * feature_rows)
 
-    def gather_row(r):
-        spots = []
-        for ref in (own_ref, got_ref):
-            numbers = ref[r, width + points :].astype(jnp.float32).astype(jnp.int32)
-            spots.append(spots_of(numbers[:SAMPLES], numbers[SAMPLES:]))
-        weights = [ref[r, width : width + points] for ref in (own_ref, got_ref)]
-        bev = [ref[r, :width] for ref in (own_ref, got_ref)]
-        return (
-            jnp.concatenate(spots, -1),
-            jnp.concatenate(weights, -1).astype(jnp.float32),
-            jnp.concatenate(bev, 0).astype(jnp.float32).T,
-        )
-
-    def sample(sampled, state, s):
-        spots, weights, _ = state
-        chosen = jnp.where(line == spots[s : s + 1, :], 1.0, 0.0).astype(jnp.bfloat16)
-        picked = jnp.dot(table, chosen, preferred_element_type=jnp.float32)
+    def sample(ref, r, first, sampled, side):
+        numbers = ref[r, points:].astype(jnp.float32).astype(jnp.int32)
+        spots = spots_of(numbers[:SAMPLES], numbers[SAMPLES:]).astype(jnp.int16)
+        weights = ref[r, :points].astype(jnp.float32)
+        for s in range(SAMPLES):
+            chosen = jnp.where(
+                line[first:] == spots[s : s + 1, :], jnp.bfloat16(1.0), jnp.bfloat16(0.0)
+            )
+            picked = jnp.dot(table[:, first:], chosen, preferred_element_type=jnp.float32)
+            for h in range(HEADS):
+                row = h * SAMPLES + s
+                term = picked[h * HEAD : (h + 1) * HEAD] * weights[row : row + 1, :]
+                sampled[h] = term if sampled[h] is None else sampled[h] + term
         for h in range(HEADS):
-            row = h * SAMPLES + s
-            term = picked[h * HEAD : (h + 1) * HEAD] * weights[row : row + 1, :]
-            sampled[h] = term if s == 0 else sampled[h] + term
-
-    def cross(sampled, state):
-        sampled = jnp.concatenate([part.astype(jnp.bfloat16) for part in sampled], 0)
+            out_ref[r, h * HEAD : (h + 1) * HEAD, side * width : (side + 1) * width] = sampled[
+                h
+            ].astype(out_ref.dtype)
+
+    for r in range(kept):
+        if not rest:
+            sample(own_ref, r, 0, [None] * HEADS, 0)
+        else:
+            other_ref, before_ref = rest
+            before = [before_ref[r, h * HEAD : (h + 1) * HEAD] for h in range(HEADS)]
+            sample(own_ref, r, known * size, before, 0)
+            sample(other_ref, r, 0, [None] * HEADS, 1)
+
+
+def row_kernel(
+    sampled_ref,
+    bev_ref,
+    got_ref,
+    cross_ref,
+    project_ref,
+    output_ref,
+    gains_ref,
+    out_ref,
+    score_scratch,
+):
+    kept, width = got_ref.shape[:2]
+    group = lax.axis_index("ba")
+    gains = jnp.concatenate([gains_ref[...], gains_ref[...]], 0).T
+    cells = 2 * width
+    rows = range(kept)
+
+    def cross(r):
+        bev = jnp.concatenate([bev_ref[group * kept + r], got_ref[r]], 0)
         after_cross = norm_columns(
-            state[2] + project(cross_ref[...], sampled), gains[:, 0:1]
+            bev.astype(jnp.float32).T + project(cross_ref[...], sampled_ref[r]), gains[:, 0:1]
         ).astype(jnp.bfloat16)
         projected = project(project_ref[...], after_cross)
         query = (projected[:C] * SCALE).astype(jnp.bfloat16)
@@ -278,24 +288,19 @@
             slot = group if piece == 0 else 1 - group
             out_ref[:, pl.ds(slot, 1), r] = blocks[:, None]
 
-    state = gather_row(0)
-    sampled = [None] * HEADS
-    for s in range(SAMPLES):
-        sample(sampled, state, s)
-    for r in range(kept):
-        parts = cross(sampled, state)
-        if r + 1 < kept:
-            state = gather_row(r + 1)
-            sampled = [None] * HEADS
-        score(parts, 0, 0)
-        mixed = []
-        for h in range(HEADS):
-            if h + 1 < HEADS:
-                score(parts, h + 1, (h + 1) % 2)
-            if r + 1 < kept:
-                sample(sampled, state, h)
-            mixed.append(mix(parts, h, h % 2))
-        finish(parts, mixed, r)
+    parts = [cross(r) for r in rows]
+    turns = [(h, r) for h in range(HEADS) for r in rows]
+    slots = score_scratch.shape[0]
+    mixed = [[] for _ in rows]
+    for turn in range(len(turns) + 1):
+        if turn < len(turns):
+            h, r = turns[turn]
+            score(parts[r], h, turn % slots)
+        if turn > 0:
+            h, r = turns[turn - 1]
+            mixed[r].append(mix(parts[r], h, (turn - 1) % slots))
+    for r in rows:
+        finish(parts[r], mixed[r], r)
 
 
 def column_kernel(
@@ -419,35 +424,42 @@
     whole = pl.BlockSpec(memory_space=pltpu.VMEM)
     params = pltpu.CompilerParams(vmem_limit_bytes=24 * 1024 * 1024)
 
-    packed = jax.ShapeDtypeStruct((kept_rows, width + (HEADS + 2) * SAMPLES, C), jnp.bfloat16)
+    packed = jax.ShapeDtypeStruct((kept_rows, (HEADS + 2) * SAMPLES, width), jnp.bfloat16)
     sent, own = pl.pallas_call(
         pack_kernel,
         out_shape=(packed, packed),
-        in_specs=[pl.BlockSpec(memory_space=pltpu.HBM)] * 5,
+        in_specs=[pl.BlockSpec(memory_space=pltpu.HBM)] * 4,
         out_specs=(whole, whole),
         scratch_shapes=[
             pltpu.VMEM((3, local_rows, SAMPLES, width), jnp.int32),
-            pltpu.SemaphoreType.DMA((7,)),
+            pltpu.SemaphoreType.DMA((5,)),
         ],
         compiler_params=pltpu.CompilerParams(vmem_limit_bytes=58 * 1024 * 1024),
         name="pack",
     )(
-        bev_query,
         sample_weight.transpose(0, 2, 3, 1).reshape(local_rows, HEADS * SAMPLES, width),
         jnp.swapaxes(camera_ids, 1, 2),
         jnp.swapaxes(level_ids, 1, 2),
         jnp.swapaxes(sample_index, 1, 2),
     )
-    got = lax.ppermute(sent, "ba", [(0, 1), (1, 0)])
+    swap = [(0, 1), (1, 0)]
 
     stages = exchange_order(band_count, group_count)
 
     def send(array, offset):
         return lax.ppermute(array, axes, [(i, i ^ offset) for i in range(device_count)])
 
-    held = jnp.concatenate([features] + [send(features, offset) for offset in stages[0][1:]], 0)
+    arrived = [send(features, offset) for offset in stages[0][1:]]
+    other = 1 - lax.axis_index("ba")
+    bev_sent = lax.dynamic_slice_in_dim(bev_query, other * kept_rows, kept_rows, 0)
+    own = own.astype(jnp.float32)
+    sent, own, bev_sent, *arrived = lax.optimization_barrier((sent, own, bev_sent, *arrived))
+    got = lax.ppermute(sent, "ba", swap)
+    bev_got = lax.ppermute(bev_sent, "ba", swap)
+    held = jnp.concatenate([features] + arrived, 0)
     tables = [held] + [send(held, offset) for offset in stages[1][1:]]
-    tables = tables + [send(table, stages[2][1]) for table in tables]
+    sides = len(tables)
+    tables.append(send(held, stages[2][1]))
 
     order = [0]
     for offsets in stages:
@@ -456,27 +468,50 @@
         order.index(1 << bit) for bit in range(device_count.bit_length() - 1)
     )
 
+    def sample(pieces, known, dtype, *cells):
+        count = width * (2 if known else 1)
+        rows = sum(tables[piece].shape[0] for piece in pieces)
+        return pl.pallas_call(
+            functools.partial(
+                sample_kernel,
+                pieces=pieces,
+                known=known,
+                map_cells=map_cells,
+                feature_rows=feature_rows,
+                place_bits=place_bits,
+            ),
+            out_shape=jax.ShapeDtypeStruct((kept_rows, C, count), dtype),
+            in_specs=[whole] * (1 + len(pieces) + len(cells)),
+            out_specs=whole,
+            compiler_params=params,
+            cost_estimate=pl.CostEstimate(
+                flops=2 * rows * kept_rows * count * SAMPLES * C,
+                bytes_accessed=8 * kept_rows * count * C,
+                transcendentals=0,
+            ),
+            name="sample",
+        )(value_weight, *[tables[piece] for piece in pieces], *cells)
+
+    near = (0, sides)
+    started = sample(near, 0, jnp.float32, own)
+    started, *tables[1:sides] = lax.optimization_barrier((started, *tables[1:sides]))
+    tables += [send(table, stages[2][1]) for table in tables[1:sides]]
+
+    far = tuple(piece for piece in range(len(tables)) if piece not in near)
+    sampled = sample(near + far, len(near), jnp.bfloat16, own, got, started)
     sent_shape = (band_count, group_count, kept_rows, column_count, C)
     after_rows = pl.pallas_call(
-        functools.partial(
-            row_kernel,
-            table_count=len(tables),
-            width=width,
-            map_cells=map_cells,
-            feature_rows=feature_rows,
-            place_bits=place_bits,
-        ),
+        row_kernel,
         out_shape=jax.ShapeDtypeStruct(sent_shape, jnp.bfloat16),
-        in_specs=[whole] * (len(tables) + 7),
+        in_specs=[whole] * 7,
         out_specs=whole,
-        scratch_shapes=[pltpu.VMEM((2, 2 * width, 2 * width), jnp.float32)],
+        scratch_shapes=[pltpu.VMEM((3, 2 * width, 2 * width), jnp.float32)],
         compiler_params=params,
         name="rows",
     )(
-        own,
-        got,
-        *tables,
-        value_weight,
+        sampled,
+        bev_query,
+        bev_got,
         cross_weight,
         row_project,
         row_output,
@@ -535,9 +570,14 @@
     out_specs = P("aa", "ba", None)
 
     def encode(*args):
-        body = fast_device if fits(mesh, args[0]) else general_device
-        return jax.shard_map(
+        fast = fits(mesh, args[0])
+
+        def body(*parts):
+            return (fast_device if fast else general_device)(*parts)
+
+        program = jax.shard_map(
             body, mesh=mesh, in_specs=in_specs, out_specs=out_specs, check_vma=False
-        )(*args)
+        )
+        return program(*args)
 
     return encode

time: 82.1 us -> 79.2 us (0.965)
  blocking collectives: 38.5 us -> 35.8 us
  Pallas kernels: 20.5 us -> 19.5 us
  other arithmetic: 0 us -> 0.9 us
    ppermute x10, waiting for transfers between devices: 9.34 us -> 5.43 us  [send(): lax.ppermute(array, axes, [(i, i ^ offset) for i in range(device_count)])]
    ppermute x1 -> x2, waiting for transfers between devices: 0.01 us -> 3.29 us  [the longest x1 3.29 us: fast_device(): got = lax.ppermute(sent, 'ba', swap)]
    all_to_all x1, blocking collectives: 20.6 us -> 17.9 us  [fast_device(): lax.all_to_all(after_rows.reshape(device_count, kept_rows * column_count,...]
    dynamic_slice x0 -> x1, local copies, waits for them, and re-layouts: none -> 0.97 us  [fast_device(): lax.dynamic_slice_in_dim(bev_query, other * kept_rows, kept_rows, 0)]
    unnamed x25 -> x27, local copies, waits for them, and re-layouts: 1.03 us -> 0.08 us
    convert_element_type x0 -> x1, other arithmetic: none -> 0.9 us  [fast_device(): own = own.astype(jnp.float32)]
    pallas_call x1 -> x3, Pallas kernels: 14.8 us -> 14.2 us  [the longest x2 7.89 us: sample(): pl.pallas_call(functools.partial(sample_kernel, pieces=pieces, known=know...]
    ppermute x1 -> x2, starting transfers between devices: 1.8 us -> 2.03 us  [the longest x1 1.5 us: fast_device(): got = lax.ppermute(sent, 'ba', swap)]
  transfers between devices with their start and end apart: 11 -> 12, of which waited for: 5 -> 5; matrix products, arithmetic and copies ran while one was open for 0% -> 2% of each run, Pallas kernels for 3% -> 12%
where the time goes in v3:
time: 79.2 us; the launch traced here: 79 us
  blocking collectives  35.8 us (45%)
  Pallas kernels  19.5 us (25%)
  starting transfers between devices  11.8 us (15%)
  waiting for transfers between devices  8.73 us (11%)
  local copies, waits for them, and re-layouts  1.89 us (2%)
  other arithmetic  0.9 us (1%)
    all_to_all x1, blocking collectives, fast_device(): lax.all_to_all(encoded.reshape(band_count, local_rows, column_count, C),...  18 us
    all_to_all x1, blocking collectives, fast_device(): lax.all_to_all(after_rows.reshape(device_count, kept_rows * column_count,...  17.9 us
    ppermute x10, starting transfers between devices, send(): lax.ppermute(array, axes, [(i, i ^ offset) for i in range(device_count)])  9.78 us
    pallas_call x2, Pallas kernels, sample(): pl.pallas_call(functools.partial(sample_kernel, pieces=pieces, known=know...  7.89 us
    pallas_call x1, Pallas kernels, fast_device(): pl.pallas_call(row_kernel, out_shape=jax.ShapeDtypeStruct(sent_shape, jnp...  6.36 us
    ppermute x10, waiting for transfers between devices, send(): lax.ppermute(array, axes, [(i, i ^ offset) for i in range(device_count)])  5.43 us
    pallas_call x1, Pallas kernels, fast_device(): pl.pallas_call(functools.partial(column_kernel, column_count=column_count...  3.67 us
    ppermute x1, waiting for transfers between devices, fast_device(): got = lax.ppermute(sent, 'ba', swap)  3.29 us
  transfers between devices with their start and end apart: 12, of which 5 were waited for; matrix products, arithmetic and copies ran while one was open for 2% of the time, Pallas kernels for 12%

profile of v3, /device:TPU:0, one launch (start us, length us, event | category | flops | bytes accessed | tf_op | source)
XLA Modules:
  0.0 79.0 jit_solution(13452210873876692110)
XLA Ops:
  0.0 4.1 %collective-permute-start.1 = (bf16[48,256]{1,0:T(8,128)(2,1)}, bf16[48,256]{1,0:T(8,128)(2,1)S(1)}, u32[]{:S(2)}, u32[]{:S(2)}) collective-permute-start(bf16[48,256]{1,0:T(8,128)(2,1)} %param.16), channel_id=1, source_target_pairs={{0,16},{1,17},{2,18},{3,19},{4,20},{5,21},{6,22},{7,23},{8,24},{9,... | collective-permute-start | bytes 73736 | tf_op jit(solution)/shard_map/ppermute | solution.py:450
  4.1 1.6 %collective-permute-start = (bf16[48,256]{1,0:T(8,128)(2,1)}, bf16[48,256]{1,0:T(8,128)(2,1)S(1)}, u32[]{:S(2)}, u32[]{:S(2)}) collective-permute-start(bf16[48,256]{1,0:T(8,128)(2,1)} %param.16), channel_id=1, source_target_pairs={{0,8},{1,9},{2,10},{3,11},{4,12},{5,13},{6,14},{7,15},{8,0},{9,1},... | collective-permute-start | bytes 73736 | tf_op jit(solution)/shard_map/ppermute | solution.py:450
  5.6 1.0 %constant_dynamic-slice_fusion = bf16[2,256,256]{2,1,0:T(8,128)(2,1)S(1)} fusion(bf16[4,256,256]{2,1,0:T(8,128)(2,1)} %bev_ref.1, s32[]{:T(128)S(6)} %select_n.3), kind=kLoop, calls=%fused_computation.4 | loop fusion | bytes 524292 | tf_op jit(solution)/shard_map/dynamic_slice | solution.py:454
  6.6 1.6 %pack.1 = (bf16[2,80,256]{2,1,0:T(8,128)(2,1)}, bf16[2,80,256]{2,1,0:T(8,128)(2,1)}) custom-call(bf16[4,64,256]{2,1,0:T(8,128)(2,1)} %bitcast.15, s32[4,8,256]{2,1,0:T(8,128)} %bitcast.16, s32[4,8,256]{2,1,0:T(8,128)} %bitcast.17, s32[4,8,256]{2,1,0:T(8,128)} %bitcast.18), custom_call_target="tpu_custom_call" | custom-call | tf_op jit(solution)/shard_map/pack/pallas_call | solution.py:428
  8.3 0.9 %convert_element_type.3.refs_2_.refs_8_ = f32[2,80,256]{2,1,0:T(8,128)S(1)} convert(bf16[2,80,256]{2,1,0:T(8,128)(2,1)} %get-tuple-element.18) | non-fusion elementwise | flops 40960 | bytes 245760 | tf_op jit(solution)/shard_map/convert_element_type | solution.py:455
  9.2 2.3 %collective-permute-done.2 = bf16[48,256]{1,0:T(8,128)(2,1)S(1)} collective-permute-done((bf16[48,256]{1,0:T(8,128)(2,1)}, bf16[48,256]{1,0:T(8,128)(2,1)S(1)}, u32[]{:S(2)}, u32[]{:S(2)}) %collective-permute-start.2) | collective-permute-done | bytes 24608 | tf_op jit(solution)/shard_map/ppermute | solution.py:450
  11.5 0.1 collective-permute-start.3
  11.6 2.5 %collective-permute-start.6 = (bf16[192,256]{1,0:T(8,128)(2,1)S(1)}, bf16[192,256]{1,0:T(8,128)(2,1)S(1)}, u32[]{:S(2)}, u32[]{:S(2)}) collective-permute-start(bf16[192,256]{1,0:T(8,128)(2,1)S(1)} %constant_dynamic-update-slice_fusion.refs_0_), channel_id=1, source_target_pairs={{0,5},{1,4},{2,7},{3,6},{4,1},{5,0},{6,3},{7,2},{8,13},{9,12},{10,... | collective-permute-start | bytes 294920 | tf_op jit(solution)/shard_map/ppermute | solution.py:450
  14.1 0.5 collective-permute-start.5
  14.6 0.5 collective-permute-start.4
  15.1 1.5 %sample.2.refs_10_ = f32[2,256,256]{2,1,0:T(8,128)S(1)} custom-call(bf16[256,256]{1,0:T(8,128)(2,1)S(1)} %copy-done.9, bf16[192,256]{1,0:T(8,128)(2,1)S(1)} %constant_dynamic-update-slice_fusion.refs_0_, bf16[192,256]{1,0:T(8,128)(2,1)S(1)} %collective-permute-done.3.refs_1_, f32[2,80,256]{2,1,0:T(8,128)S(1)} %convert_element_type.3.refs_2_.refs_8_), custom_call_target="tpu_custom_call" | custom-call | flops 805306368 | bytes 1048576 | tf_op jit(solution)/shard_map/sample/pallas_call | solution.py:474
  16.7 1.1 %collective-permute-done.6.refs_4_ = bf16[192,256]{1,0:T(8,128)(2,1)S(1)} collective-permute-done((bf16[192,256]{1,0:T(8,128)(2,1)S(1)}, bf16[192,256]{1,0:T(8,128)(2,1)S(1)}, u32[]{:S(2)}, u32[]{:S(2)}) %collective-permute-start.6) | collective-permute-done | bytes 98336 | tf_op jit(solution)/shard_map/ppermute | solution.py:450
  17.8 2.0 %collective-permute-done.5.refs_3_ = bf16[192,256]{1,0:T(8,128)(2,1)S(1)} collective-permute-done((bf16[192,256]{1,0:T(8,128)(2,1)S(1)}, bf16[192,256]{1,0:T(8,128)(2,1)S(1)}, u32[]{:S(2)}, u32[]{:S(2)}) %collective-permute-start.5) | collective-permute-done | bytes 98336 | tf_op jit(solution)/shard_map/ppermute | solution.py:450
  19.8 0.1 collective-permute-done.4.refs_2_
  19.8 0.5 collective-permute-start.8
  20.4 1.5 %collective-permute-start.10 = (bf16[2,80,256]{2,1,0:T(8,128)(2,1)S(1)}, bf16[2,80,256]{2,1,0:T(8,128)(2,1)S(1)}, u32[]{:S(2)}, u32[]{:S(2)}) collective-permute-start(bf16[2,80,256]{2,1,0:T(8,128)(2,1)S(1)} %copy-done.11), channel_id=1, source_target_pairs={{0,1},{1,0},{2,3},{3,2},{4,5},{5,4},{6,7},{7,6},{8,9},{9,8},{10,11... | collective-permute-start | bytes 245768 | tf_op jit(solution)/shard_map/ppermute | solution.py:457
  21.9 0.5 collective-permute-start.11
  22.4 3.3 %collective-permute-done.10.refs_9_ = bf16[2,80,256]{2,1,0:T(8,128)(2,1)S(1)} collective-permute-done((bf16[2,80,256]{2,1,0:T(8,128)(2,1)S(1)}, bf16[2,80,256]{2,1,0:T(8,128)(2,1)S(1)}, u32[]{:S(2)}, u32[]{:S(2)}) %collective-permute-start.10) | collective-permute-done | bytes 81952 | tf_op jit(solution)/shard_map/ppermute | solution.py:457
  25.7 6.4 %sample.3.sampled_ref = bf16[2,256,512]{2,1,0:T(8,128)(2,1)S(1)} custom-call(bf16[256,256]{1,0:T(8,128)(2,1)S(1)} %copy-done.9, bf16[192,256]{1,0:T(8,128)(2,1)S(1)} %constant_dynamic-update-slice_fusion.refs_0_, bf16[192,256]{1,0:T(8,128)(2,1)S(1)} %collective-permute-done.3.refs_1_, bf16[192,256]{1,0:T(8,128)(2,1)S(1)} %collective-permute-done.4.refs_2_, ...), custom_call_target="tpu_custom_call" | custom-call | flops 6442450944 | bytes 2097152 | tf_op jit(solution)/shard_map/sample/pallas_call | solution.py:474
  32.2 6.4 %rows.1 = bf16[16,2,2,16,256]{4,3,2,1,0:T(8,128)(2,1)S(1)} custom-call(bf16[2,256,512]{2,1,0:T(8,128)(2,1)S(1)} %sample.3.sampled_ref, bf16[4,256,256]{2,1,0:T(8,128)(2,1)S(1)} %copy-done, bf16[2,256,256]{2,1,0:T(8,128)(2,1)S(1)} %collective-permute-done.11.got_ref, bf16[256,256]{1,0:T(8,128)(2,1)S(1)} %copy-done.5, bf16[256,768]{1,0:T(8,128)(2,1)S(1)} %copy-done.1, ...), custom_call_target="tpu_custom_call" | custom-call | tf_op jit(solution)/shard_map/rows/pallas_call | solution.py:503
  38.6 17.9 %all_to_all.10 = bf16[32,32,256]{2,1,0:T(8,128)(2,1)S(1)} all-to-all(bf16[32,32,256]{2,1,0:T(8,128)(2,1)S(1)} %bitcast.11), channel_id=1, replica_groups=mesh['aa'=16,'ba'=2] {'aa','ba'}, dimensions={0} | all-to-all | bytes 1048576 | tf_op jit(solution)/shard_map/all_to_all | solution.py:520
  56.5 3.7 %columns.1 = bf16[1024,256]{1,0:T(8,128)(2,1)S(1)} custom-call(bf16[1024,256]{1,0:T(8,128)(2,1)S(1)} %bitcast.12, bf16[256,768]{1,0:T(8,128)(2,1)S(1)} %copy-done.2, bf16[256,256]{1,0:T(8,128)(2,1)S(1)} %copy-done.7, bf16[256,512]{1,0:T(8,128)(2,1)S(1)} %copy-done.3, bf16[512,256]{1,0:T(8,128)(2,1)S(1)} %copy-done.4, f32[4,256]{1,0:T(4,128)S(1)} %copy-done.8), custom_call_target="tpu_custom_call" | custom-call | tf_op jit(solution)/shard_map/columns/pallas_call | solution.py:523
  60.2 18.0 %all_to_all.11 = bf16[16,4,16,256]{3,2,1,0:T(8,128)(2,1)S(1)} all-to-all(bf16[16,4,16,256]{3,2,1,0:T(8,128)(2,1)S(1)} %bitcast.13), channel_id=1, replica_groups=mesh['aa'=16,'ba'=2] {'aa'}, dimensions={0} | all-to-all | bytes 1048576 | tf_op jit(solution)/shard_map/all_to_all | solution.py:532
  78.1 0.8 %copy.16 = bf16[4,16,16,256]{3,2,1,0:T(8,128)(2,1)} copy(bf16[4,16,16,256]{3,2,0,1:T(8,128)(2,1)S(1)} %bitcast.14) | data formatting | bytes 1048576 | tf_op jit(solution)/shard_map/transpose | solution.py:535
  (38 shorter events, 0.1 us)
Async XLA Ops:
  0.0 9.2 %collective-permute-start.1 = (bf16[48,256]{1,0:T(8,128)(2,1)}, bf16[48,256]{1,0:T(8,128)(2,1)S(1)}, u32[]{:S(2)}, u32[]{:S(2)}) collective-permute-start(bf16[48,256]{1,0:T(8,128)(2,1)} %param.16), channel_id=1, source_target_pairs={{0,16},{1,17},{2,18},{3,19},{4,20},{5,21},{6,22},{7,23},{8,24},{9,... | collective-permute-start | bytes 73736 | tf_op jit(solution)/shard_map/ppermute | solution.py:450
  4.1 5.1 %collective-permute-start = (bf16[48,256]{1,0:T(8,128)(2,1)}, bf16[48,256]{1,0:T(8,128)(2,1)S(1)}, u32[]{:S(2)}, u32[]{:S(2)}) collective-permute-start(bf16[48,256]{1,0:T(8,128)(2,1)} %param.16), channel_id=1, source_target_pairs={{0,8},{1,9},{2,10},{3,11},{4,12},{5,13},{6,14},{7,15},{8,0},{9,1},... | collective-permute-start | bytes 73736 | tf_op jit(solution)/shard_map/ppermute | solution.py:450
  5.6 5.8 %collective-permute-start.2 = (bf16[48,256]{1,0:T(8,128)(2,1)}, bf16[48,256]{1,0:T(8,128)(2,1)S(1)}, u32[]{:S(2)}, u32[]{:S(2)}) collective-permute-start(bf16[48,256]{1,0:T(8,128)(2,1)} %param.16), channel_id=1, source_target_pairs={{0,24},{1,25},{2,26},{3,27},{4,28},{5,29},{6,30},{7,31},{8,16},{9,... | collective-permute-start | bytes 73736 | tf_op jit(solution)/shard_map/ppermute | solution.py:450
  5.6 1.0 %copy-start.10 = (bf16[48,256]{1,0:T(8,128)(2,1)S(1)}, bf16[48,256]{1,0:T(8,128)(2,1)}, u32[]{:S(2)}) copy-start(bf16[48,256]{1,0:T(8,128)(2,1)} %param.16) | copy-start | bytes 73732
  9.2 6.0 %copy-start.9 = (bf16[256,256]{1,0:T(8,128)(2,1)S(1)}, bf16[256,256]{1,0:T(8,128)(2,1)}, u32[]{:S(2)}) copy-start(bf16[256,256]{1,0:T(8,128)(2,1)} %value_weight_ref.3) | copy-start | bytes 393220
  11.5 8.9 %copy-start.11 = (bf16[2,80,256]{2,1,0:T(8,128)(2,1)S(1)}, bf16[2,80,256]{2,1,0:T(8,128)(2,1)}, u32[]{:S(2)}) copy-start(bf16[2,80,256]{2,1,0:T(8,128)(2,1)} %get-tuple-element.26) | copy-start | bytes 245764
  11.5 3.6 %collective-permute-start.3 = (bf16[192,256]{1,0:T(8,128)(2,1)S(1)}, bf16[192,256]{1,0:T(8,128)(2,1)S(1)}, u32[]{:S(2)}, u32[]{:S(2)}) collective-permute-start(bf16[192,256]{1,0:T(8,128)(2,1)S(1)} %constant_dynamic-update-slice_fusion.refs_0_), channel_id=1, source_target_pairs={{0,2},{1,3},{2,0},{3,1},{4,6},{5,7},{6,4},{7,5},{8,10},{9,11},{10,... | collective-permute-start | bytes 294920 | tf_op jit(solution)/shard_map/ppermute | solution.py:450
  11.6 6.2 %collective-permute-start.6 = (bf16[192,256]{1,0:T(8,128)(2,1)S(1)}, bf16[192,256]{1,0:T(8,128)(2,1)S(1)}, u32[]{:S(2)}, u32[]{:S(2)}) collective-permute-start(bf16[192,256]{1,0:T(8,128)(2,1)S(1)} %constant_dynamic-update-slice_fusion.refs_0_), channel_id=1, source_target_pairs={{0,5},{1,4},{2,7},{3,6},{4,1},{5,0},{6,3},{7,2},{8,13},{9,12},{10,... | collective-permute-start | bytes 294920 | tf_op jit(solution)/shard_map/ppermute | solution.py:450
  14.1 5.7 %collective-permute-start.5 = (bf16[192,256]{1,0:T(8,128)(2,1)S(1)}, bf16[192,256]{1,0:T(8,128)(2,1)S(1)}, u32[]{:S(2)}, u32[]{:S(2)}) collective-permute-start(bf16[192,256]{1,0:T(8,128)(2,1)S(1)} %constant_dynamic-update-slice_fusion.refs_0_), channel_id=1, source_target_pairs={{0,1},{1,0},{2,3},{3,2},{4,5},{5,4},{6,7},{7,6},{8,9},{9,8},{10,11... | collective-permute-start | bytes 294920 | tf_op jit(solution)/shard_map/ppermute | solution.py:450
  14.6 5.2 %collective-permute-start.4 = (bf16[192,256]{1,0:T(8,128)(2,1)S(1)}, bf16[192,256]{1,0:T(8,128)(2,1)S(1)}, u32[]{:S(2)}, u32[]{:S(2)}) collective-permute-start(bf16[192,256]{1,0:T(8,128)(2,1)S(1)} %constant_dynamic-update-slice_fusion.refs_0_), channel_id=1, source_target_pairs={{0,4},{1,5},{2,6},{3,7},{4,0},{5,1},{6,2},{7,3},{8,12},{9,13},{10,... | collective-permute-start | bytes 294920 | tf_op jit(solution)/shard_map/ppermute | solution.py:450
  16.6 15.5 %copy-start = (bf16[4,256,256]{2,1,0:T(8,128)(2,1)S(1)}, bf16[4,256,256]{2,1,0:T(8,128)(2,1)}, u32[]{:S(2)}) copy-start(bf16[4,256,256]{2,1,0:T(8,128)(2,1)} %bev_ref.1) | copy-start | bytes 1572868
  16.6 15.5 %copy-start.1 = (bf16[256,768]{1,0:T(8,128)(2,1)S(1)}, bf16[256,768]{1,0:T(8,128)(2,1)}, u32[]{:S(2)}) copy-start(bf16[256,768]{1,0:T(8,128)(2,1)} %project_ref.2) | copy-start | bytes 1179652
  16.6 15.5 %copy-start.5 = (bf16[256,256]{1,0:T(8,128)(2,1)S(1)}, bf16[256,256]{1,0:T(8,128)(2,1)}, u32[]{:S(2)}) copy-start(bf16[256,256]{1,0:T(8,128)(2,1)} %cross_ref.1) | copy-start | bytes 393220
  16.7 15.5 %copy-start.6 = (bf16[256,256]{1,0:T(8,128)(2,1)S(1)}, bf16[256,256]{1,0:T(8,128)(2,1)}, u32[]{:S(2)}) copy-start(bf16[256,256]{1,0:T(8,128)(2,1)} %output_ref.2) | copy-start | bytes 393220
  16.7 15.5 %copy-start.8 = (f32[4,256]{1,0:T(4,128)S(1)}, f32[4,256]{1,0:T(4,128)}, u32[]{:S(2)}) copy-start(f32[4,256]{1,0:T(4,128)} %gains_ref.3) | copy-start | bytes 12292
  19.8 5.8 %collective-permute-start.7 = (bf16[192,256]{1,0:T(8,128)(2,1)S(1)}, bf16[192,256]{1,0:T(8,128)(2,1)S(1)}, u32[]{:S(2)}, u32[]{:S(2)}) collective-permute-start(bf16[192,256]{1,0:T(8,128)(2,1)S(1)} %collective-permute-done.4.refs_2_), channel_id=1, source_target_pairs={{0,2},{1,3},{2,0},{3,1},{4,6},{5,7},{6,4},{7,5},{8,10},{9,11},{10,... | collective-permute-start | bytes 294920 | tf_op jit(solution)/shard_map/ppermute | solution.py:450
  19.8 5.8 %collective-permute-start.8 = (bf16[192,256]{1,0:T(8,128)(2,1)S(1)}, bf16[192,256]{1,0:T(8,128)(2,1)S(1)}, u32[]{:S(2)}, u32[]{:S(2)}) collective-permute-start(bf16[192,256]{1,0:T(8,128)(2,1)S(1)} %collective-permute-done.5.refs_3_), channel_id=1, source_target_pairs={{0,2},{1,3},{2,0},{3,1},{4,6},{5,7},{6,4},{7,5},{8,10},{9,11},{10,... | collective-permute-start | bytes 294920 | tf_op jit(solution)/shard_map/ppermute | solution.py:450
  20.4 5.3 %collective-permute-start.9 = (bf16[192,256]{1,0:T(8,128)(2,1)S(1)}, bf16[192,256]{1,0:T(8,128)(2,1)S(1)}, u32[]{:S(2)}, u32[]{:S(2)}) collective-permute-start(bf16[192,256]{1,0:T(8,128)(2,1)S(1)} %collective-permute-done.6.refs_4_), channel_id=1, source_target_pairs={{0,2},{1,3},{2,0},{3,1},{4,6},{5,7},{6,4},{7,5},{8,10},{9,11},{10,... | collective-permute-start | bytes 294920 | tf_op jit(solution)/shard_map/ppermute | solution.py:450
  20.4 5.3 %collective-permute-start.10 = (bf16[2,80,256]{2,1,0:T(8,128)(2,1)S(1)}, bf16[2,80,256]{2,1,0:T(8,128)(2,1)S(1)}, u32[]{:S(2)}, u32[]{:S(2)}) collective-permute-start(bf16[2,80,256]{2,1,0:T(8,128)(2,1)S(1)} %copy-done.11), channel_id=1, source_target_pairs={{0,1},{1,0},{2,3},{3,2},{4,5},{5,4},{6,7},{7,6},{8,9},{9,8},{10,11... | collective-permute-start | bytes 245768 | tf_op jit(solution)/shard_map/ppermute | solution.py:457
  21.9 10.3 %collective-permute-start.11 = (bf16[2,256,256]{2,1,0:T(8,128)(2,1)S(1)}, bf16[2,256,256]{2,1,0:T(8,128)(2,1)S(1)}, u32[]{:S(2)}, u32[]{:S(2)}) collective-permute-start(bf16[2,256,256]{2,1,0:T(8,128)(2,1)S(1)} %constant_dynamic-slice_fusion), channel_id=1, source_target_pairs={{0,1},{1,0},{2,3},{3,2},{4,5},{5,4},{6,7},{7,6},{8,9},{9,8},{10,11... | collective-permute-start | bytes 786440 | tf_op jit(solution)/shard_map/ppermute | solution.py:458
  38.5 17.9 %copy-start.2 = (bf16[256,768]{1,0:T(8,128)(2,1)S(1)}, bf16[256,768]{1,0:T(8,128)(2,1)}, u32[]{:S(2)}) copy-start(bf16[256,768]{1,0:T(8,128)(2,1)} %project_ref.3) | copy-start | bytes 1179652
  38.6 17.9 %copy-start.3 = (bf16[256,512]{1,0:T(8,128)(2,1)S(1)}, bf16[256,512]{1,0:T(8,128)(2,1)}, u32[]{:S(2)}) copy-start(bf16[256,512]{1,0:T(8,128)(2,1)} %expand_ref.1) | copy-start | bytes 786436
  38.6 17.9 %copy-start.4 = (bf16[512,256]{1,0:T(8,128)(2,1)S(1)}, bf16[512,256]{1,0:T(8,128)(2,1)}, u32[]{:S(2)}) copy-start(bf16[512,256]{1,0:T(8,128)(2,1)} %reduce_ref.1) | copy-start | bytes 786436
  38.6 17.9 %copy-start.7 = (bf16[256,256]{1,0:T(8,128)(2,1)S(1)}, bf16[256,256]{1,0:T(8,128)(2,1)}, u32[]{:S(2)}) copy-start(bf16[256,256]{1,0:T(8,128)(2,1)} %output_ref.3) | copy-start | bytes 393220

commit v4 on v3

--- a/solution.py
+++ b/solution.py
@@ -270,7 +270,8 @@
         mixed = []
         for start in range(0, cells, 2 * LANES):
             scores = score_scratch[slot, :, start : start + 2 * LANES]
-            powers = jnp.exp2(scores - jnp.max(scores, 0, keepdims=True))
+            most = jnp.max(scores.reshape(8, -1, 2 * LANES), 0)
+            powers = jnp.exp2(scores - jnp.max(most, 0, keepdims=True))
             product = jnp.dot(
                 with_ones(values), powers.astype(jnp.bfloat16), preferred_element_type=jnp.float32
             )
@@ -292,13 +293,13 @@
     turns = [(h, r) for h in range(HEADS) for r in rows]
     slots = score_scratch.shape[0]
     mixed = [[] for _ in rows]
-    for turn in range(len(turns) + 1):
+    for turn in range(len(turns) + 2):
         if turn < len(turns):
             h, r = turns[turn]
             score(parts[r], h, turn % slots)
-        if turn > 0:
-            h, r = turns[turn - 1]
-            mixed[r].append(mix(parts[r], h, (turn - 1) % slots))
+        if turn > 1:
+            h, r = turns[turn - 2]
+            mixed[r].append(mix(parts[r], h, (turn - 2) % slots))
     for r in rows:
         finish(parts[r], mixed[r], r)
 
@@ -505,7 +506,7 @@
         out_shape=jax.ShapeDtypeStruct(sent_shape, jnp.bfloat16),
         in_specs=[whole] * 7,
         out_specs=whole,
-        scratch_shapes=[pltpu.VMEM((3, 2 * width, 2 * width), jnp.float32)],
+        scratch_shapes=[pltpu.VMEM((4, 2 * width, 2 * width), jnp.float32)],
         compiler_params=params,
         name="rows",
     )(

time: 79.2 us -> 78.9 us (level)
  no operation moved by 1% of the time
where the time goes in v4:
time: 78.9 us; the launch traced here: 78.6 us
  blocking collectives  35.8 us (45%)
  Pallas kernels  19.2 us (24%)
  starting transfers between devices  11.8 us (15%)
  waiting for transfers between devices  8.73 us (11%)
  local copies, waits for them, and re-layouts  1.89 us (2%)
  other arithmetic  0.9 us (1%)
    all_to_all x1, blocking collectives, fast_device(): lax.all_to_all(encoded.reshape(band_count, local_rows, column_count, C),...  18 us
    all_to_all x1, blocking collectives, fast_device(): lax.all_to_all(after_rows.reshape(device_count, kept_rows * column_count,...  17.9 us
    ppermute x10, starting transfers between devices, send(): lax.ppermute(array, axes, [(i, i ^ offset) for i in range(device_count)])  9.78 us
    pallas_call x2, Pallas kernels, sample(): pl.pallas_call(functools.partial(sample_kernel, pieces=pieces, known=know...  7.89 us
    pallas_call x1, Pallas kernels, fast_device(): pl.pallas_call(row_kernel, out_shape=jax.ShapeDtypeStruct(sent_shape, jnp...  6.05 us
    ppermute x10, waiting for transfers between devices, send(): lax.ppermute(array, axes, [(i, i ^ offset) for i in range(device_count)])  5.43 us
    pallas_call x1, Pallas kernels, fast_device(): pl.pallas_call(functools.partial(column_kernel, column_count=column_count...  3.67 us
    ppermute x1, waiting for transfers between devices, fast_device(): got = lax.ppermute(sent, 'ba', swap)  3.29 us
  transfers between devices with their start and end apart: 12, of which 5 were waited for; matrix products, arithmetic and copies ran while one was open for 2% of the time, Pallas kernels for 12%

profile of v4, /device:TPU:0, one launch (start us, length us, event | category | flops | bytes accessed | tf_op | source)
XLA Modules:
  0.0 78.6 jit_solution(4400967715298675092)
XLA Ops:
  0.0 4.1 %collective-permute-start.1 = (bf16[48,256]{1,0:T(8,128)(2,1)}, bf16[48,256]{1,0:T(8,128)(2,1)S(1)}, u32[]{:S(2)}, u32[]{:S(2)}) collective-permute-start(bf16[48,256]{1,0:T(8,128)(2,1)} %param.16), channel_id=1, source_target_pairs={{0,16},{1,17},{2,18},{3,19},{4,20},{5,21},{6,22},{7,23},{8,24},{9,... | collective-permute-start | bytes 73736 | tf_op jit(solution)/shard_map/ppermute | solution.py:451
  4.1 1.6 %collective-permute-start = (bf16[48,256]{1,0:T(8,128)(2,1)}, bf16[48,256]{1,0:T(8,128)(2,1)S(1)}, u32[]{:S(2)}, u32[]{:S(2)}) collective-permute-start(bf16[48,256]{1,0:T(8,128)(2,1)} %param.16), channel_id=1, source_target_pairs={{0,8},{1,9},{2,10},{3,11},{4,12},{5,13},{6,14},{7,15},{8,0},{9,1},... | collective-permute-start | bytes 73736 | tf_op jit(solution)/shard_map/ppermute | solution.py:451
  5.6 1.0 %constant_dynamic-slice_fusion = bf16[2,256,256]{2,1,0:T(8,128)(2,1)S(1)} fusion(bf16[4,256,256]{2,1,0:T(8,128)(2,1)} %bev_ref.1, s32[]{:T(128)S(6)} %select_n.3), kind=kLoop, calls=%fused_computation.4 | loop fusion | bytes 524292 | tf_op jit(solution)/shard_map/dynamic_slice | solution.py:455
  6.6 1.6 %pack.1 = (bf16[2,80,256]{2,1,0:T(8,128)(2,1)}, bf16[2,80,256]{2,1,0:T(8,128)(2,1)}) custom-call(bf16[4,64,256]{2,1,0:T(8,128)(2,1)} %bitcast.15, s32[4,8,256]{2,1,0:T(8,128)} %bitcast.16, s32[4,8,256]{2,1,0:T(8,128)} %bitcast.17, s32[4,8,256]{2,1,0:T(8,128)} %bitcast.18), custom_call_target="tpu_custom_call" | custom-call | tf_op jit(solution)/shard_map/pack/pallas_call | solution.py:429
  8.3 0.9 %convert_element_type.3.refs_2_.refs_8_ = f32[2,80,256]{2,1,0:T(8,128)S(1)} convert(bf16[2,80,256]{2,1,0:T(8,128)(2,1)} %get-tuple-element.18) | non-fusion elementwise | flops 40960 | bytes 245760 | tf_op jit(solution)/shard_map/convert_element_type | solution.py:456
  9.2 2.3 %collective-permute-done.2 = bf16[48,256]{1,0:T(8,128)(2,1)S(1)} collective-permute-done((bf16[48,256]{1,0:T(8,128)(2,1)}, bf16[48,256]{1,0:T(8,128)(2,1)S(1)}, u32[]{:S(2)}, u32[]{:S(2)}) %collective-permute-start.2) | collective-permute-done | bytes 24608 | tf_op jit(solution)/shard_map/ppermute | solution.py:451
  11.5 0.1 collective-permute-start.3
  11.6 2.5 %collective-permute-start.6 = (bf16[192,256]{1,0:T(8,128)(2,1)S(1)}, bf16[192,256]{1,0:T(8,128)(2,1)S(1)}, u32[]{:S(2)}, u32[]{:S(2)}) collective-permute-start(bf16[192,256]{1,0:T(8,128)(2,1)S(1)} %constant_dynamic-update-slice_fusion.refs_0_), channel_id=1, source_target_pairs={{0,5},{1,4},{2,7},{3,6},{4,1},{5,0},{6,3},{7,2},{8,13},{9,12},{10,... | collective-permute-start | bytes 294920 | tf_op jit(solution)/shard_map/ppermute | solution.py:451
  14.1 0.5 collective-permute-start.5
  14.6 0.5 collective-permute-start.4
  15.1 1.5 %sample.2.refs_10_ = f32[2,256,256]{2,1,0:T(8,128)S(1)} custom-call(bf16[256,256]{1,0:T(8,128)(2,1)S(1)} %copy-done.9, bf16[192,256]{1,0:T(8,128)(2,1)S(1)} %constant_dynamic-update-slice_fusion.refs_0_, bf16[192,256]{1,0:T(8,128)(2,1)S(1)} %collective-permute-done.3.refs_1_, f32[2,80,256]{2,1,0:T(8,128)S(1)} %convert_element_type.3.refs_2_.refs_8_), custom_call_target="tpu_custom_call" | custom-call | flops 805306368 | bytes 1048576 | tf_op jit(solution)/shard_map/sample/pallas_call | solution.py:475
  16.7 1.1 %collective-permute-done.6.refs_4_ = bf16[192,256]{1,0:T(8,128)(2,1)S(1)} collective-permute-done((bf16[192,256]{1,0:T(8,128)(2,1)S(1)}, bf16[192,256]{1,0:T(8,128)(2,1)S(1)}, u32[]{:S(2)}, u32[]{:S(2)}) %collective-permute-start.6) | collective-permute-done | bytes 98336 | tf_op jit(solution)/shard_map/ppermute | solution.py:451
  17.8 2.0 %collective-permute-done.5.refs_3_ = bf16[192,256]{1,0:T(8,128)(2,1)S(1)} collective-permute-done((bf16[192,256]{1,0:T(8,128)(2,1)S(1)}, bf16[192,256]{1,0:T(8,128)(2,1)S(1)}, u32[]{:S(2)}, u32[]{:S(2)}) %collective-permute-start.5) | collective-permute-done | bytes 98336 | tf_op jit(solution)/shard_map/ppermute | solution.py:451
  19.8 0.1 collective-permute-done.4.refs_2_
  19.8 0.5 collective-permute-start.8
  20.4 1.5 %collective-permute-start.10 = (bf16[2,80,256]{2,1,0:T(8,128)(2,1)S(1)}, bf16[2,80,256]{2,1,0:T(8,128)(2,1)S(1)}, u32[]{:S(2)}, u32[]{:S(2)}) collective-permute-start(bf16[2,80,256]{2,1,0:T(8,128)(2,1)S(1)} %copy-done.11), channel_id=1, source_target_pairs={{0,1},{1,0},{2,3},{3,2},{4,5},{5,4},{6,7},{7,6},{8,9},{9,8},{10,11... | collective-permute-start | bytes 245768 | tf_op jit(solution)/shard_map/ppermute | solution.py:458
  21.9 0.5 collective-permute-start.11
  22.4 3.3 %collective-permute-done.10.refs_9_ = bf16[2,80,256]{2,1,0:T(8,128)(2,1)S(1)} collective-permute-done((bf16[2,80,256]{2,1,0:T(8,128)(2,1)S(1)}, bf16[2,80,256]{2,1,0:T(8,128)(2,1)S(1)}, u32[]{:S(2)}, u32[]{:S(2)}) %collective-permute-start.10) | collective-permute-done | bytes 81952 | tf_op jit(solution)/shard_map/ppermute | solution.py:458
  25.7 6.4 %sample.3.sampled_ref = bf16[2,256,512]{2,1,0:T(8,128)(2,1)S(1)} custom-call(bf16[256,256]{1,0:T(8,128)(2,1)S(1)} %copy-done.9, bf16[192,256]{1,0:T(8,128)(2,1)S(1)} %constant_dynamic-update-slice_fusion.refs_0_, bf16[192,256]{1,0:T(8,128)(2,1)S(1)} %collective-permute-done.3.refs_1_, bf16[192,256]{1,0:T(8,128)(2,1)S(1)} %collective-permute-done.4.refs_2_, ...), custom_call_target="tpu_custom_call" | custom-call | flops 6442450944 | bytes 2097152 | tf_op jit(solution)/shard_map/sample/pallas_call | solution.py:475
  32.2 6.0 %rows.1 = bf16[16,2,2,16,256]{4,3,2,1,0:T(8,128)(2,1)S(1)} custom-call(bf16[2,256,512]{2,1,0:T(8,128)(2,1)S(1)} %sample.3.sampled_ref, bf16[4,256,256]{2,1,0:T(8,128)(2,1)S(1)} %copy-done, bf16[2,256,256]{2,1,0:T(8,128)(2,1)S(1)} %collective-permute-done.11.got_ref, bf16[256,256]{1,0:T(8,128)(2,1)S(1)} %copy-done.5, bf16[256,768]{1,0:T(8,128)(2,1)S(1)} %copy-done.1, ...), custom_call_target="tpu_custom_call" | custom-call | tf_op jit(solution)/shard_map/rows/pallas_call | solution.py:504
  38.3 17.9 %all_to_all.10 = bf16[32,32,256]{2,1,0:T(8,128)(2,1)S(1)} all-to-all(bf16[32,32,256]{2,1,0:T(8,128)(2,1)S(1)} %bitcast.11), channel_id=1, replica_groups=mesh['aa'=16,'ba'=2] {'aa','ba'}, dimensions={0} | all-to-all | bytes 1048576 | tf_op jit(solution)/shard_map/all_to_all | solution.py:521
  56.2 3.7 %columns.1 = bf16[1024,256]{1,0:T(8,128)(2,1)S(1)} custom-call(bf16[1024,256]{1,0:T(8,128)(2,1)S(1)} %bitcast.12, bf16[256,768]{1,0:T(8,128)(2,1)S(1)} %copy-done.2, bf16[256,256]{1,0:T(8,128)(2,1)S(1)} %copy-done.7, bf16[256,512]{1,0:T(8,128)(2,1)S(1)} %copy-done.3, bf16[512,256]{1,0:T(8,128)(2,1)S(1)} %copy-done.4, f32[4,256]{1,0:T(4,128)S(1)} %copy-done.8), custom_call_target="tpu_custom_call" | custom-call | tf_op jit(solution)/shard_map/columns/pallas_call | solution.py:524
  59.8 18.0 %all_to_all.11 = bf16[16,4,16,256]{3,2,1,0:T(8,128)(2,1)S(1)} all-to-all(bf16[16,4,16,256]{3,2,1,0:T(8,128)(2,1)S(1)} %bitcast.13), channel_id=1, replica_groups=mesh['aa'=16,'ba'=2] {'aa'}, dimensions={0} | all-to-all | bytes 1048576 | tf_op jit(solution)/shard_map/all_to_all | solution.py:533
  77.8 0.8 %copy.16 = bf16[4,16,16,256]{3,2,1,0:T(8,128)(2,1)} copy(bf16[4,16,16,256]{3,2,0,1:T(8,128)(2,1)S(1)} %bitcast.14) | data formatting | bytes 1048576 | tf_op jit(solution)/shard_map/transpose | solution.py:536
  (38 shorter events, 0.1 us)
Async XLA Ops:
  0.0 9.2 %collective-permute-start.1 = (bf16[48,256]{1,0:T(8,128)(2,1)}, bf16[48,256]{1,0:T(8,128)(2,1)S(1)}, u32[]{:S(2)}, u32[]{:S(2)}) collective-permute-start(bf16[48,256]{1,0:T(8,128)(2,1)} %param.16), channel_id=1, source_target_pairs={{0,16},{1,17},{2,18},{3,19},{4,20},{5,21},{6,22},{7,23},{8,24},{9,... | collective-permute-start | bytes 73736 | tf_op jit(solution)/shard_map/ppermute | solution.py:451
  4.1 5.1 %collective-permute-start = (bf16[48,256]{1,0:T(8,128)(2,1)}, bf16[48,256]{1,0:T(8,128)(2,1)S(1)}, u32[]{:S(2)}, u32[]{:S(2)}) collective-permute-start(bf16[48,256]{1,0:T(8,128)(2,1)} %param.16), channel_id=1, source_target_pairs={{0,8},{1,9},{2,10},{3,11},{4,12},{5,13},{6,14},{7,15},{8,0},{9,1},... | collective-permute-start | bytes 73736 | tf_op jit(solution)/shard_map/ppermute | solution.py:451
  5.6 5.8 %collective-permute-start.2 = (bf16[48,256]{1,0:T(8,128)(2,1)}, bf16[48,256]{1,0:T(8,128)(2,1)S(1)}, u32[]{:S(2)}, u32[]{:S(2)}) collective-permute-start(bf16[48,256]{1,0:T(8,128)(2,1)} %param.16), channel_id=1, source_target_pairs={{0,24},{1,25},{2,26},{3,27},{4,28},{5,29},{6,30},{7,31},{8,16},{9,... | collective-permute-start | bytes 73736 | tf_op jit(solution)/shard_map/ppermute | solution.py:451
  5.6 1.0 %copy-start.10 = (bf16[48,256]{1,0:T(8,128)(2,1)S(1)}, bf16[48,256]{1,0:T(8,128)(2,1)}, u32[]{:S(2)}) copy-start(bf16[48,256]{1,0:T(8,128)(2,1)} %param.16) | copy-start | bytes 73732
  9.2 6.0 %copy-start.9 = (bf16[256,256]{1,0:T(8,128)(2,1)S(1)}, bf16[256,256]{1,0:T(8,128)(2,1)}, u32[]{:S(2)}) copy-start(bf16[256,256]{1,0:T(8,128)(2,1)} %value_weight_ref.3) | copy-start | bytes 393220
  11.5 8.9 %copy-start.11 = (bf16[2,80,256]{2,1,0:T(8,128)(2,1)S(1)}, bf16[2,80,256]{2,1,0:T(8,128)(2,1)}, u32[]{:S(2)}) copy-start(bf16[2,80,256]{2,1,0:T(8,128)(2,1)} %get-tuple-element.26) | copy-start | bytes 245764
  11.5 3.6 %collective-permute-start.3 = (bf16[192,256]{1,0:T(8,128)(2,1)S(1)}, bf16[192,256]{1,0:T(8,128)(2,1)S(1)}, u32[]{:S(2)}, u32[]{:S(2)}) collective-permute-start(bf16[192,256]{1,0:T(8,128)(2,1)S(1)} %constant_dynamic-update-slice_fusion.refs_0_), channel_id=1, source_target_pairs={{0,2},{1,3},{2,0},{3,1},{4,6},{5,7},{6,4},{7,5},{8,10},{9,11},{10,... | collective-permute-start | bytes 294920 | tf_op jit(solution)/shard_map/ppermute | solution.py:451
  11.6 6.2 %collective-permute-start.6 = (bf16[192,256]{1,0:T(8,128)(2,1)S(1)}, bf16[192,256]{1,0:T(8,128)(2,1)S(1)}, u32[]{:S(2)}, u32[]{:S(2)}) collective-permute-start(bf16[192,256]{1,0:T(8,128)(2,1)S(1)} %constant_dynamic-update-slice_fusion.refs_0_), channel_id=1, source_target_pairs={{0,5},{1,4},{2,7},{3,6},{4,1},{5,0},{6,3},{7,2},{8,13},{9,12},{10,... | collective-permute-start | bytes 294920 | tf_op jit(solution)/shard_map/ppermute | solution.py:451
  14.1 5.7 %collective-permute-start.5 = (bf16[192,256]{1,0:T(8,128)(2,1)S(1)}, bf16[192,256]{1,0:T(8,128)(2,1)S(1)}, u32[]{:S(2)}, u32[]{:S(2)}) collective-permute-start(bf16[192,256]{1,0:T(8,128)(2,1)S(1)} %constant_dynamic-update-slice_fusion.refs_0_), channel_id=1, source_target_pairs={{0,1},{1,0},{2,3},{3,2},{4,5},{5,4},{6,7},{7,6},{8,9},{9,8},{10,11... | collective-permute-start | bytes 294920 | tf_op jit(solution)/shard_map/ppermute | solution.py:451
  14.6 5.2 %collective-permute-start.4 = (bf16[192,256]{1,0:T(8,128)(2,1)S(1)}, bf16[192,256]{1,0:T(8,128)(2,1)S(1)}, u32[]{:S(2)}, u32[]{:S(2)}) collective-permute-start(bf16[192,256]{1,0:T(8,128)(2,1)S(1)} %constant_dynamic-update-slice_fusion.refs_0_), channel_id=1, source_target_pairs={{0,4},{1,5},{2,6},{3,7},{4,0},{5,1},{6,2},{7,3},{8,12},{9,13},{10,... | collective-permute-start | bytes 294920 | tf_op jit(solution)/shard_map/ppermute | solution.py:451
  16.6 15.5 %copy-start = (bf16[4,256,256]{2,1,0:T(8,128)(2,1)S(1)}, bf16[4,256,256]{2,1,0:T(8,128)(2,1)}, u32[]{:S(2)}) copy-start(bf16[4,256,256]{2,1,0:T(8,128)(2,1)} %bev_ref.1) | copy-start | bytes 1572868
  16.6 15.5 %copy-start.1 = (bf16[256,768]{1,0:T(8,128)(2,1)S(1)}, bf16[256,768]{1,0:T(8,128)(2,1)}, u32[]{:S(2)}) copy-start(bf16[256,768]{1,0:T(8,128)(2,1)} %project_ref.2) | copy-start | bytes 1179652
  16.6 15.5 %copy-start.5 = (bf16[256,256]{1,0:T(8,128)(2,1)S(1)}, bf16[256,256]{1,0:T(8,128)(2,1)}, u32[]{:S(2)}) copy-start(bf16[256,256]{1,0:T(8,128)(2,1)} %cross_ref.1) | copy-start | bytes 393220
  16.7 15.5 %copy-start.6 = (bf16[256,256]{1,0:T(8,128)(2,1)S(1)}, bf16[256,256]{1,0:T(8,128)(2,1)}, u32[]{:S(2)}) copy-start(bf16[256,256]{1,0:T(8,128)(2,1)} %output_ref.2) | copy-start | bytes 393220
  16.7 15.5 %copy-start.8 = (f32[4,256]{1,0:T(4,128)S(1)}, f32[4,256]{1,0:T(4,128)}, u32[]{:S(2)}) copy-start(f32[4,256]{1,0:T(4,128)} %gains_ref.3) | copy-start | bytes 12292
  19.8 5.8 %collective-permute-start.7 = (bf16[192,256]{1,0:T(8,128)(2,1)S(1)}, bf16[192,256]{1,0:T(8,128)(2,1)S(1)}, u32[]{:S(2)}, u32[]{:S(2)}) collective-permute-start(bf16[192,256]{1,0:T(8,128)(2,1)S(1)} %collective-permute-done.4.refs_2_), channel_id=1, source_target_pairs={{0,2},{1,3},{2,0},{3,1},{4,6},{5,7},{6,4},{7,5},{8,10},{9,11},{10,... | collective-permute-start | bytes 294920 | tf_op jit(solution)/shard_map/ppermute | solution.py:451
  19.8 5.8 %collective-permute-start.8 = (bf16[192,256]{1,0:T(8,128)(2,1)S(1)}, bf16[192,256]{1,0:T(8,128)(2,1)S(1)}, u32[]{:S(2)}, u32[]{:S(2)}) collective-permute-start(bf16[192,256]{1,0:T(8,128)(2,1)S(1)} %collective-permute-done.5.refs_3_), channel_id=1, source_target_pairs={{0,2},{1,3},{2,0},{3,1},{4,6},{5,7},{6,4},{7,5},{8,10},{9,11},{10,... | collective-permute-start | bytes 294920 | tf_op jit(solution)/shard_map/ppermute | solution.py:451
  20.4 5.3 %collective-permute-start.9 = (bf16[192,256]{1,0:T(8,128)(2,1)S(1)}, bf16[192,256]{1,0:T(8,128)(2,1)S(1)}, u32[]{:S(2)}, u32[]{:S(2)}) collective-permute-start(bf16[192,256]{1,0:T(8,128)(2,1)S(1)} %collective-permute-done.6.refs_4_), channel_id=1, source_target_pairs={{0,2},{1,3},{2,0},{3,1},{4,6},{5,7},{6,4},{7,5},{8,10},{9,11},{10,... | collective-permute-start | bytes 294920 | tf_op jit(solution)/shard_map/ppermute | solution.py:451
  20.4 5.3 %collective-permute-start.10 = (bf16[2,80,256]{2,1,0:T(8,128)(2,1)S(1)}, bf16[2,80,256]{2,1,0:T(8,128)(2,1)S(1)}, u32[]{:S(2)}, u32[]{:S(2)}) collective-permute-start(bf16[2,80,256]{2,1,0:T(8,128)(2,1)S(1)} %copy-done.11), channel_id=1, source_target_pairs={{0,1},{1,0},{2,3},{3,2},{4,5},{5,4},{6,7},{7,6},{8,9},{9,8},{10,11... | collective-permute-start | bytes 245768 | tf_op jit(solution)/shard_map/ppermute | solution.py:458
  21.9 10.3 %collective-permute-start.11 = (bf16[2,256,256]{2,1,0:T(8,128)(2,1)S(1)}, bf16[2,256,256]{2,1,0:T(8,128)(2,1)S(1)}, u32[]{:S(2)}, u32[]{:S(2)}) collective-permute-start(bf16[2,256,256]{2,1,0:T(8,128)(2,1)S(1)} %constant_dynamic-slice_fusion), channel_id=1, source_target_pairs={{0,1},{1,0},{2,3},{3,2},{4,5},{5,4},{6,7},{7,6},{8,9},{9,8},{10,11... | collective-permute-start | bytes 786440 | tf_op jit(solution)/shard_map/ppermute | solution.py:459
  38.2 17.9 %copy-start.2 = (bf16[256,768]{1,0:T(8,128)(2,1)S(1)}, bf16[256,768]{1,0:T(8,128)(2,1)}, u32[]{:S(2)}) copy-start(bf16[256,768]{1,0:T(8,128)(2,1)} %project_ref.3) | copy-start | bytes 1179652
  38.2 17.9 %copy-start.3 = (bf16[256,512]{1,0:T(8,128)(2,1)S(1)}, bf16[256,512]{1,0:T(8,128)(2,1)}, u32[]{:S(2)}) copy-start(bf16[256,512]{1,0:T(8,128)(2,1)} %expand_ref.1) | copy-start | bytes 786436
  38.3 17.9 %copy-start.4 = (bf16[512,256]{1,0:T(8,128)(2,1)S(1)}, bf16[512,256]{1,0:T(8,128)(2,1)}, u32[]{:S(2)}) copy-start(bf16[512,256]{1,0:T(8,128)(2,1)} %reduce_ref.1) | copy-start | bytes 786436
  38.3 17.9 %copy-start.7 = (bf16[256,256]{1,0:T(8,128)(2,1)S(1)}, bf16[256,256]{1,0:T(8,128)(2,1)}, u32[]{:S(2)}) copy-start(bf16[256,256]{1,0:T(8,128)(2,1)} %output_ref.3) | copy-start | bytes 393220
